TPU v7x, 32 devices: a whole 2x2x4 slice. The times are simulated.
32 devices in a mesh: gx: 2 (over y), gy: 4 (over x, core), gz: 4 (over z).
Axes of the slice: x: 2, y: 2, z: 4, core: 2. Of those that a mesh axis runs over, the one named last changes fastest.
Arguments:
- probe_bits: int32 [8, 32, 512], P('gx', 'gz', 'gy'), may hold values from -2147483648 to 2147483646
- disorder_levels: int32 [8, 32, 512], P('gx', 'gz', 'gy'), may hold values from -2147483648 to 2147483647, as said below
Outputs:
- moments: float32 [3, 8], replicated
- previous: float32 [8, 8, 128, 512], P(None, 'gx', 'gz', 'gy')
- current: float32 [8, 8, 128, 512], P(None, 'gx', 'gz', 'gy')
Inputs may be any that keep to these rules, and one draw needn't show every extreme that they name: `disorder_levels`: every byte of a word is a level 0 to 255.
All inputs are finite; a program needn't handle non-finite values.
Results may differ from a plain program's by a relative error of at most 0.00002.
Values sent between devices are 32-bit elements; how exact they have to be, the bound alone decides.
A program may use at most 64 MiB of HBM per device.

v0:
```python
import functools

import jax
import jax.numpy as jnp
from jax import lax
from jax.experimental import pallas as pl
from jax.experimental.pallas import tpu as pltpu
from jax.sharding import PartitionSpec as P

PROBES = 8
LEVELS = 256
LANES = 128
SITES = 4
STRIP = 12

disorder_width = 4.0
spectral_scale = 8.4
MESH = pl.DeviceIdType.MESH


def kernel(names, sizes, p_hbm, d_hbm, prow_hbm, drow_hbm, mom_ref, prev_ref, cur_ref,
           p_ref, d_ref, words, packs, strips, v0, v1, v2, en, s0, s1, s2, se, moms,
           load_sem, send_sem, recv_sem, msend_sem, mrecv_sem):
    X, W, _ = p_ref.shape
    Z = SITES * W
    nbx = packs.shape[0]
    M = nbx * X
    gx, gy, gz = sizes["gx"], sizes["gy"], sizes["gz"]
    ix, iy, iz = (lax.axis_index(a) for a in ("gx", "gy", "gz"))
    total = gx * gy * gz
    me = (ix * gy + iy) * gz + iz

    def device(x, y, z):
        at = {"gx": x, "gy": y, "gz": z}
        return tuple(at[a] for a in names)

    loads = [pltpu.make_async_copy(src, dst, load_sem.at[n]) for n, (src, dst) in enumerate((
        (p_hbm, p_ref), (d_hbm, d_ref),
        (prow_hbm, words.at[0, pl.ds(0, X), pl.ds(1, W)]), (drow_hbm, words.at[1, pl.ds(0, X), pl.ds(1, W)])))]
    for load in loads:
        load.start()

    def around(at, size):
        steps = [at]
        for _ in range(size - 1):
            steps.append(jnp.where(steps[-1] + 1 == size, 0, steps[-1] + 1))
        return steps

    around_x, around_y = around(ix, gx), around(iy, gy)

    def each_other(act):
        for x in range(gx):
            for y in range(gy):
                if x or y:
                    act(device(around_x[x], around_y[y], iz))

        def at_depth(z):
            for x in range(gx):
                for y in range(gy):
                    act(device(around_x[x], around_y[y], z))

        if gz <= 4:
            for z in around(iz, gz)[1:]:
                at_depth(z)
        else:
            def step(k, _):
                at_depth(lax.rem(iz + k, gz))
                return 0
            lax.fori_loop(1, gz, step, 0)

    barrier = pltpu.get_barrier_semaphore()
    each_other(lambda to: pl.semaphore_signal(barrier, inc=1, device_id=to, device_id_type=MESH))

    lane = lax.broadcasted_iota(jnp.int32, (2 * X, LANES), 1)
    slot_word = (lane * 10923) >> 17
    column = lane - STRIP * slot_word

    for load in loads:
        load.wait()
    pack = jnp.zeros((2 * X, LANES), jnp.int32)
    for w in range(W):
        rows = jnp.concatenate([p_ref[:, w, :], d_ref[:, w, :]], axis=0)
        base = STRIP * (w + 1)
        first = pltpu.roll(rows, (base - (LANES - 3)) % LANES, 1)
        second = pltpu.roll(rows, (base + 5 - (LANES - 2)) % LANES, 1)
        pack = jnp.where(slot_word == w + 1, jnp.where(column < 5, first, second), pack)
    packs[0, 1, 1] = pack

    pl.semaphore_wait(barrier, total - 1)

    xs = (1, 0) if nbx == 2 else (1, -1, 0)
    near, far = [], []
    slot_of = {0: 0, 1: nbx - 1, -1: 1}
    for ox in xs:
        for oz in (0, 1, -1):
            for oy in (0, 1, -1):
                if ox == 0 and oz == 0 and oy == 0:
                    continue
                to = device(lax.rem(ix + ox + gx, gx), lax.rem(iy + oy + gy, gy), lax.rem(iz + oz + gz, gz))
                s = slot_of[ox]
                moves = []
                if oy == 0:
                    src_w, dst_w = {0: (pl.ds(1, W), pl.ds(1, W)), 1: (pl.ds(W, 1), pl.ds(0, 1)),
                                    -1: (pl.ds(1, 1), pl.ds(W + 1, 1))}[oz]
                    for f in range(2):
                        moves.append((words.at[f, pl.ds(0, X), src_w], words.at[f, pl.ds(s * X, X), dst_w]))
                moves.append((packs.at[0, 1, 1], packs.at[s, 1 - oz, 1 - oy]))
                for src, dst in moves:
                    n = len(near) + len(far)
                    (far if ox else near).append(pltpu.make_async_remote_copy(
                        src_ref=src, dst_ref=dst, send_sem=send_sem.at[n], recv_sem=recv_sem.at[n],
                        device_id=to, device_id_type=MESH))
    for copy in far + near:
        copy.start()
    scale = 1.0 / spectral_scale
    e_mul = disorder_width / LEVELS / spectral_scale
    e_add = disorder_width * (0.5 / LEVELS - 0.5) / spectral_scale
    probe = lax.broadcasted_iota(jnp.int32, (PROBES, LANES), 0)
    lane8 = lax.broadcasted_iota(jnp.int32, (PROBES, LANES), 1)
    col8 = lane8 - STRIP * ((lane8 * 10923) >> 17)
    lifts = [31 - (SITES * probe + j) for j in range(SITES)]

    def sign_of(row, j):
        return jnp.where((jnp.broadcast_to(row, (PROBES, LANES)) << lifts[j]) < 0, 1.0, -1.0).astype(jnp.float32)

    def energy_of(row, j):
        level = (jnp.broadcast_to(row, (PROBES, LANES)) >> (8 * j)) & 255
        return level.astype(jnp.float32) * e_mul + e_add

    def unpack(q, zs):
        for z in zs:
            w, j = divmod(z + SITES, SITES)
            v0[q, z + 3] = sign_of(words[0, q, w], j)
            en[q, z + 3] = energy_of(words[1, q, w], j)

    def unpack_own(x, _):
        unpack(x, range(Z))
        return 0

    lax.fori_loop(0, X, unpack_own, 0)
    for copy in near:
        copy.wait()

    def unpack_strips(s):
        def joined(oz):
            return jnp.where(column < 3, packs[s, oz, 0], jnp.where(column < 7, packs[s, oz, 1], packs[s, oz, 2]))
        strip = jnp.where(slot_word == 0, pltpu.roll(joined(0), (-STRIP * W) % LANES, 1), joined(1))
        strips[s] = jnp.where(slot_word == W + 1, pltpu.roll(joined(2), (STRIP * W) % LANES, 1), strip)
        for x in range(X):
            for j in range(SITES):
                s0[s * X + x, j] = sign_of(strips[s, x:x + 1], j)
                se[s * X + x, j] = energy_of(strips[s, X + x:X + x + 1], j)

    def plane(e):
        return lax.rem(e + M, M)

    def unpack_rim(x, _):
        unpack(x, [*range(-3, 0), *range(Z, Z + 3)])
        return 0

    def unpack_far(i, _):
        unpack(plane(X + i), range(-3, Z + 3))
        return 0

    def unpack_low(i, _):
        unpack(plane(i - 3), range(-3, Z + 3))
        return 0

    unpack_strips(0)
    lax.fori_loop(0, X, unpack_rim, 0)

    def strip_sum(src, q, up, down):
        mine = [src[q, j] for j in range(SITES)]
        sums = []
        for j in range(SITES):
            z_up = mine[j + 1] if j + 1 < SITES else pltpu.roll(mine[0], LANES - STRIP, 1)
            z_down = mine[j - 1] if j > 0 else pltpu.roll(mine[SITES - 1], STRIP, 1)
            sums.append(src[up, j] + src[down, j] + pltpu.roll(mine[j], LANES - 1, 1)
                        + pltpu.roll(mine[j], 1, 1) + z_up + z_down)
        return mine, sums

    def edges_of(mine):
        return [jnp.where(col8 == 1, pltpu.roll(m, LANES - 6, 1), m) for m in mine]

    def site_sum(src, q, up, down, z, edges):
        w, j = divmod(z + SITES, SITES)
        fix = pltpu.roll(edges[j], (-(STRIP * w + 2)) % LANES, 1)
        mid = src[q, z + 3]
        right = jnp.where(lane8 == LANES - 1, fix, pltpu.roll(mid, LANES - 1, 1))
        left = jnp.where(lane8 == 0, fix, pltpu.roll(mid, 1, 1))
        return mid, src[up, z + 3] + src[down, z + 3] + right + left + src[q, z + 4] + src[q, z + 2]

    zero = jnp.zeros((PROBES, LANES), jnp.float32)

    def first_level(e, accs):
        q, up, down = plane(e), plane(e + 1), plane(e + M - 1)
        mine, sums = strip_sum(s0, q, up, down)
        for j in range(SITES):
            s1[q, j] = se[q, j] * mine[j] - scale * sums[j]
        edges = edges_of(mine)
        one, two = zero, zero
        for z in range(-2, Z + 2):
            mid, total_six = site_sum(v0, q, up, down, z, edges)
            new = en[q, z + 3] * mid - scale * total_six
            v1[q, z + 3] = new
            if 0 <= z < Z:
                one, two = one + mid * new, two + new * new
        return accs[0] + one, accs[1] + two

    def first_edge(e):
        def body(i, accs):
            return first_level(i * (X - 1) + e * (1 - 2 * i), accs)
        return body

    accs = lax.fori_loop(1, X - 1, first_level, (zero, zero))
    for copy in far:
        copy.wait()
    for s in range(1, nbx):
        unpack_strips(s)
    if M <= X + 6:
        lax.fori_loop(0, M - X, unpack_far, 0)
    else:
        lax.fori_loop(0, 3, unpack_far, 0)
        lax.fori_loop(0, 3, unpack_low, 0)
    m1, m2 = lax.fori_loop(0, 2, first_edge(0), accs)
    lax.fori_loop(0, 2, first_edge(-1), (zero, zero))

    def second_level(e, acc):
        q, up, down = plane(e), plane(e + 1), plane(e + M - 1)
        mine, sums = strip_sum(s1, q, up, down)
        for j in range(SITES):
            s2[q, j] = 2.0 * (se[q, j] * mine[j] - scale * sums[j]) - s0[q, j]
        edges = edges_of(mine)
        three = zero
        for z in range(-1, Z + 1):
            mid, total_six = site_sum(v1, q, up, down, z, edges)
            new = 2.0 * (en[q, z + 3] * mid - scale * total_six) - v0[q, z + 3]
            v2[q, z + 3] = new
            if 0 <= z < Z:
                three = three + mid * new
        return acc + three

    m3 = lax.fori_loop(0, X, second_level, zero)

    row = zero
    for n, acc in enumerate((m1, m2, m3)):
        summed = jnp.broadcast_to(jnp.sum(acc, axis=1, keepdims=True), (PROBES, LANES))
        row = row + jnp.where(lane8 == PROBES * n + probe, summed, 0.0)
    moms[me] = jnp.sum(row, axis=0, keepdims=True)

    each_other(lambda to: pltpu.make_async_remote_copy(
        src_ref=moms.at[me], dst_ref=moms.at[me], send_sem=msend_sem, recv_sem=mrecv_sem,
        device_id=to, device_id_type=MESH).start())

    lax.fori_loop(0, min(M, X + 4) - (X + 2), first_edge(-2), (zero, zero))

    def rim_planes(i, _):
        second_level(i * (X + 1) - 1, zero)
        return 0

    lax.fori_loop(0, 2, rim_planes, 0)

    def third_level(x, _):
        q, up, down = plane(x), plane(x + 1), plane(x + M - 1)
        edges = edges_of([s2[q, j] for j in range(SITES)])
        for z in range(Z):
            mid, total_six = site_sum(v2, q, up, down, z, edges)
            new = 2.0 * (en[q, z + 3] * mid - scale * total_six) - v1[q, z + 3]
            at = pl.ds(x * Z + z, PROBES, stride=X * Z)
            prev_ref[at, :] = mid
            cur_ref[at, :] = new
        return 0

    lax.fori_loop(0, X, third_level, 0)

    others = moms.at[pl.ds(0, total - 1)]
    pltpu.make_async_copy(others, others, mrecv_sem).wait()
    pltpu.make_async_copy(others, others, msend_sem).wait()
    sites = total * X * Z * LANES
    sums = jnp.sum(moms[...], axis=0) * (1.0 / sites)
    first = sums
    second = 2.0 * pltpu.roll(sums, LANES - PROBES, 1) - 1.0
    third = 2.0 * pltpu.roll(sums, LANES - 2 * PROBES, 1) - sums
    mom_ref[...] = jnp.concatenate([first, second, third], axis=0)[:, :PROBES]


def write_out(mom_ref, prev_ref, cur_ref, mom_hbm, prev_hbm, cur_hbm, sem):
    copies = [pltpu.make_async_copy(src, dst, sem.at[n]) for n, (src, dst) in enumerate((
        (prev_ref, prev_hbm), (cur_ref, cur_hbm), (mom_ref, mom_hbm)))]
    for copy in copies:
        copy.start()
    for copy in copies:
        copy.wait()


def per_device(names, sizes, probe_bits, disorder_levels):
    X, W, Y = probe_bits.shape
    if Y != LANES or STRIP * (W + 2) > LANES or X < 3:
        raise ValueError("block size")
    Z = SITES * W
    nbx = 2 if sizes["gx"] == 2 else 3
    M = nbx * X
    n_copies = (9 * nbx - 1) + 2 * (3 * nbx - 1)
    total = sizes["gx"] * sizes["gy"] * sizes["gz"]
    rows = (X, W, 1, Y)
    vmem = pl.BlockSpec(memory_space=pltpu.VMEM)
    f32, i32 = jnp.float32, jnp.int32
    tile = (PROBES, LANES)
    hbm = pl.BlockSpec(memory_space=pltpu.HBM)
    out_shape = (
        jax.ShapeDtypeStruct((3, PROBES), f32),
        jax.ShapeDtypeStruct((PROBES * X * Z, Y), f32),
        jax.ShapeDtypeStruct((PROBES * X * Z, Y), f32),
    )
    results = pl.pallas_call(
        functools.partial(kernel, names, sizes),
        out_shape=out_shape,
        in_specs=[hbm] * 4,
        out_specs=(vmem,) * 3,
        scratch_shapes=[
            pltpu.VMEM((X, W, Y), i32),
            pltpu.VMEM((X, W, Y), i32),
            pltpu.VMEM((2, M, W + 2, 1, LANES), i32),
            pltpu.VMEM((nbx, 3, 3, 2 * X, LANES), i32),
            pltpu.VMEM((nbx, 2 * X, LANES), i32),
            pltpu.VMEM((M, Z + 6) + tile, f32),
            pltpu.VMEM((M, Z + 6) + tile, f32),
            pltpu.VMEM((M, Z + 6) + tile, f32),
            pltpu.VMEM((M, Z + 6) + tile, f32),
            pltpu.VMEM((M, SITES) + tile, f32),
            pltpu.VMEM((M, SITES) + tile, f32),
            pltpu.VMEM((M, SITES) + tile, f32),
            pltpu.VMEM((M, SITES) + tile, f32),
            pltpu.VMEM((total, 1, LANES), f32),
            pltpu.SemaphoreType.DMA((4,)),
            pltpu.SemaphoreType.DMA((n_copies,)),
            pltpu.SemaphoreType.DMA((n_copies,)),
            pltpu.SemaphoreType.DMA,
            pltpu.SemaphoreType.DMA,
        ],
        compiler_params=pltpu.CompilerParams(collective_id=0, has_side_effects=True,
                                             vmem_limit_bytes=40 * 1024 * 1024),
    )(*[pltpu.with_memory_space_constraint(a, pltpu.HBM) for a in (probe_bits, disorder_levels, probe_bits.reshape(rows), disorder_levels.reshape(rows))])
    moments, previous, current = pl.pallas_call(
        write_out,
        out_shape=out_shape,
        in_specs=[vmem] * 3,
        out_specs=(hbm,) * 3,
        scratch_shapes=[pltpu.SemaphoreType.DMA((3,))],
        compiler_params=pltpu.CompilerParams(vmem_limit_bytes=16 * 1024 * 1024),
    )(*results)
    shape = (PROBES, X, Z, Y)
    return moments, previous.reshape(shape), current.reshape(shape)


def solution(mesh):
    placed = (P("gx", "gz", "gy"), P("gx", "gz", "gy"))
    sizes = {a: mesh.shape[a] for a in mesh.axis_names}
    return jax.shard_map(
        functools.partial(per_device, tuple(mesh.axis_names), sizes),
        mesh=mesh,
        in_specs=placed,
        out_specs=(P(), P(None, "gx", "gz", "gy"), P(None, "gx", "gz", "gy")),
        check_vma=False,
    )
```

profile of v0, /device:TPU:0, one launch (start us, length us, event | category | flops | bytes accessed | tf_op | source)
XLA Modules:
  0.0 20.3 jit_solution(12506918898068162675)
XLA Ops:
  0.6 18.7 %shard_map.49 = (f32[3,8]{1,0:T(4,128)S(1)}, f32[1024,128]{1,0:T(8,128)S(1)}, f32[1024,128]{1,0:T(8,128)S(1)}) custom-call(s32[4,8,128]{2,1,0:T(8,128)} %p_hbm.1, s32[4,8,128]{2,1,0:T(8,128)} %d_hbm.1, s32[4,8,1,128]{3,2,1,0:T(1,128)} %bitcast.4, s32[4,8,1,128]{3,2,1,0:T(1,128)} %bitcast.5), custom_call_target="tpu_custom_call" | custom-call | tf_op jit(solution)/shard_map/pallas_call | solution.py:315
  19.3 1.0 %shard_map.50 = (f32[3,8]{1,0:T(4,128)}, f32[1024,128]{1,0:T(8,128)}, f32[1024,128]{1,0:T(8,128)}) custom-call(f32[3,8]{1,0:T(4,128)S(1)} %get-tuple-element.9.mom_ref, f32[1024,128]{1,0:T(8,128)S(1)} %get-tuple-element.10.prev_ref, f32[1024,128]{1,0:T(8,128)S(1)} %get-tuple-element.11.cur_ref), custom_call_target="tpu_custom_call" | custom-call | tf_op jit(solution)/shard_map/pallas_call | solution.py:344
where the time goes:
time: 20.6 us; the launch traced here: 20.3 us
  Pallas kernels  19.7 us (96%)
  between operations  0.64 us (3%)
    pallas_call x1, Pallas kernels, per_device(): pl.pallas_call(functools.partial(kernel, names, sizes), out_shape=out_sha...  18.7 us
    pallas_call x1, Pallas kernels, per_device(): pl.pallas_call(write_out, out_shape=out_shape, in_specs=[vmem] * 3, out_s...  1 us

commit v1 on v0

v1 whole, which is shorter than its diff:
```python
import functools

import jax
import jax.numpy as jnp
from jax import lax
from jax.experimental import pallas as pl
from jax.experimental.pallas import tpu as pltpu
from jax.sharding import PartitionSpec as P

PROBES = 8
LEVELS = 256
LANES = 128
SITES = 4
STRIP = 12

disorder_width = 4.0
spectral_scale = 8.4
MESH = pl.DeviceIdType.MESH


def kernel(names, sizes, p_hbm, d_hbm, prow_hbm, drow_hbm, mom_ref, prev_ref, cur_ref,
           p_ref, d_ref, words, packs, strips, v0, v1, v2, en, s0, s1, s2, se, accs, moms,
           load_sem, send_sem, recv_sem, msend_sem, mrecv_sem, token):
    X, W, _ = p_ref.shape
    Z = SITES * W
    nbx = packs.shape[0]
    M = nbx * X
    gx, gy, gz = sizes["gx"], sizes["gy"], sizes["gz"]
    ix, iy, iz = (lax.axis_index(a) for a in ("gx", "gy", "gz"))
    total = gx * gy * gz
    me = (ix * gy + iy) * gz + iz
    last = gz - 1
    staged = gx <= 3 and gy <= 4 and 3 <= gz <= 4

    def device(x, y, z):
        at = {"gx": x, "gy": y, "gz": z}
        return tuple(at[a] for a in names)

    loads = [pltpu.make_async_copy(src, dst, load_sem.at[n]) for n, (src, dst) in enumerate((
        (p_hbm, p_ref), (d_hbm, d_ref),
        (prow_hbm, words.at[0, pl.ds(0, X), pl.ds(1, W)]), (drow_hbm, words.at[1, pl.ds(0, X), pl.ds(1, W)])))]
    for load in loads:
        load.start()

    def around(at, size):
        steps = [at]
        for _ in range(size - 1):
            steps.append(jnp.where(steps[-1] + 1 == size, 0, steps[-1] + 1))
        return steps

    around_x, around_y = around(ix, gx), around(iy, gy)

    def plane_of_others(z, act):
        for x in range(gx):
            for y in range(gy):
                if x or y:
                    act(device(around_x[x], around_y[y], z))

    def whole_plane(z, act):
        for x in range(gx):
            for y in range(gy):
                act(device(around_x[x], around_y[y], z))

    def each_other(act):
        if gz <= 4:
            for z in around(iz, gz)[1:]:
                whole_plane(z, act)
        else:
            def step(k, _):
                whole_plane(lax.rem(iz + k, gz), act)
                return 0
            lax.fori_loop(1, gz, step, 0)
        plane_of_others(iz, act)

    xs = (0, 1) if nbx == 2 else (0, 1, -1)
    ys = (0, 1, -1)

    def at_offset(ox, oy, oz):
        return device(lax.rem(ix + ox + gx, gx), lax.rem(iy + oy + gy, gy), lax.rem(iz + oz + gz, gz))

    barrier = pltpu.get_barrier_semaphore()

    def greet(to):
        pl.semaphore_signal(barrier, inc=1, device_id=to, device_id_type=MESH)

    per_plane = len(xs) * len(ys)
    if staged:
        @pl.when(iz < last)
        def _():
            whole_plane(last, greet)
            for ox in xs:
                for oy in ys:
                    if ox or oy:
                        greet(at_offset(ox, oy, 0))

        @pl.when(iz == last)
        def _():
            plane_of_others(iz, greet)

        @pl.when(iz > 0)
        def _():
            for ox in xs:
                for oy in ys:
                    greet(at_offset(ox, oy, -1))

        @pl.when(iz + 1 < last)
        def _():
            for ox in xs:
                for oy in ys:
                    greet(at_offset(ox, oy, 1))
    else:
        each_other(greet)

    lane = lax.broadcasted_iota(jnp.int32, (2 * X, LANES), 1)
    slot_word = (lane * 10923) >> 17
    column = lane - STRIP * slot_word

    for load in loads:
        load.wait()
    pack = jnp.zeros((2 * X, LANES), jnp.int32)
    for w in range(W):
        rows = jnp.concatenate([p_ref[:, w, :], d_ref[:, w, :]], axis=0)
        base = STRIP * (w + 1)
        first = pltpu.roll(rows, (base - (LANES - 3)) % LANES, 1)
        second = pltpu.roll(rows, (base + 5 - (LANES - 2)) % LANES, 1)
        pack = jnp.where(slot_word == w + 1, jnp.where(column < 5, first, second), pack)
    packs[0, 1, 1] = pack

    if staged:
        @pl.when(iz == last)
        def _():
            pl.semaphore_wait(barrier, total - 1)

        @pl.when(iz == 0)
        def _():
            pl.semaphore_wait(barrier, 2 * per_plane - 1)

        @pl.when((iz > 0) & (iz < last))
        def _():
            pl.semaphore_wait(barrier, 3 * per_plane - 1)
    else:
        pl.semaphore_wait(barrier, total - 1)

    slot_of = {0: 0, 1: nbx - 1, -1: 1}
    groups = {"far": [], "near": [], 1: [], -1: []}
    count = 0
    for oz in (0, 1, -1):
        for ox in xs:
            for oy in ys:
                if ox == 0 and oz == 0 and oy == 0:
                    continue
                s = slot_of[ox]
                moves = []
                if oy == 0:
                    src_w, dst_w = {0: (pl.ds(1, W), pl.ds(1, W)), 1: (pl.ds(W, 1), pl.ds(0, 1)),
                                    -1: (pl.ds(1, 1), pl.ds(W + 1, 1))}[oz]
                    for f in range(2):
                        moves.append((words.at[f, pl.ds(0, X), src_w], words.at[f, pl.ds(s * X, X), dst_w]))
                moves.append((packs.at[0, 1, 1], packs.at[s, 1 - oz, 1 - oy]))
                for src, dst in moves:
                    groups[oz if oz else ("far" if ox else "near")].append(pltpu.make_async_remote_copy(
                        src_ref=src, dst_ref=dst, send_sem=send_sem.at[count], recv_sem=recv_sem.at[count],
                        device_id=at_offset(ox, oy, oz), device_id_type=MESH))
                    count += 1

    for copy in groups["far"] + groups[1] + groups["near"]:
        copy.start()
    if staged:
        @pl.when(iz > 0)
        def _():
            for copy in groups[-1]:
                copy.start()

        @pl.when(iz == last)
        def _():
            for ox in xs:
                for oy in ys:
                    pl.semaphore_signal(token, inc=1, device_id=at_offset(ox, oy, 1), device_id_type=MESH)
    else:
        for copy in groups[-1]:
            copy.start()

    scale = 1.0 / spectral_scale
    e_mul = disorder_width / LEVELS / spectral_scale
    e_add = disorder_width * (0.5 / LEVELS - 0.5) / spectral_scale
    probe = lax.broadcasted_iota(jnp.int32, (PROBES, LANES), 0)
    lane8 = lax.broadcasted_iota(jnp.int32, (PROBES, LANES), 1)
    slot8 = (lane8 * 10923) >> 17
    col8 = lane8 - STRIP * slot8
    lifts = [31 - (SITES * probe + j) for j in range(SITES)]
    zero = jnp.zeros((PROBES, LANES), jnp.float32)

    def ends(at, size):
        return at == 0, at != size - 1

    (low_x, high_x), (low_y, high_y), (low_z, high_z) = ends(ix, gx), ends(iy, gy), ends(iz, gz)

    def sign_of(row, j):
        return jnp.where((jnp.broadcast_to(row, (PROBES, LANES)) << lifts[j]) < 0, 1.0, -1.0).astype(jnp.float32)

    def energy_of(row, j):
        level = (jnp.broadcast_to(row, (PROBES, LANES)) >> (8 * j)) & 255
        return level.astype(jnp.float32) * e_mul + e_add

    def unpack(q, zs):
        for z in zs:
            w, j = divmod(z + SITES, SITES)
            v0[q, z + 3] = sign_of(words[0, q, w], j)
            en[q, z + 3] = energy_of(words[1, q, w], j)

    def plane(e):
        return lax.rem(e + M, M)

    def planes(low, high, body):
        def step(i, _):
            body(plane(i - low))
            return 0
        lax.fori_loop(0, min(M, X + low + high), step, 0)

    def join_strips(s, oz):
        return jnp.where(column < 3, packs[s, oz, 0], jnp.where(column < 7, packs[s, oz, 1], packs[s, oz, 2]))

    def unpack_strips(s):
        for x in range(X):
            for j in range(SITES):
                s0[s * X + x, j] = sign_of(strips[s, x:x + 1], j)
                se[s * X + x, j] = energy_of(strips[s, X + x:X + x + 1], j)

    def strip_sum(src, q, up, down):
        mine = [src[q, j] for j in range(SITES)]
        sums, rights, ups = [], [], []
        for j in range(SITES):
            z_up = mine[j + 1] if j + 1 < SITES else pltpu.roll(mine[0], LANES - STRIP, 1)
            z_down = mine[j - 1] if j > 0 else pltpu.roll(mine[SITES - 1], STRIP, 1)
            sums.append(src[up, j] + src[down, j] + pltpu.roll(mine[j], LANES - 1, 1)
                        + pltpu.roll(mine[j], 1, 1) + z_up + z_down)
        return mine, sums

    def edges_of(mine):
        return [jnp.where(col8 == 1, pltpu.roll(m, LANES - 6, 1), m) for m in mine]

    def site_sum(src, q, up, down, z, edges):
        w, j = divmod(z + SITES, SITES)
        fix = pltpu.roll(edges[j], (-(STRIP * w + 2)) % LANES, 1)
        mid = src[q, z + 3]
        right = jnp.where(lane8 == LANES - 1, fix, pltpu.roll(mid, LANES - 1, 1))
        left = jnp.where(lane8 == 0, fix, pltpu.roll(mid, 1, 1))
        return mid, src[up, z + 3] + src[down, z + 3] + right + left + src[q, z + 4] + src[q, z + 2]

    def around_plane(e):
        return plane(e), plane(e + 1), plane(e + M - 1)

    site_cols = ((col8 == 2) & low_y) | ((col8 == 7) & high_y)
    bond_cols = (((col8 == 1) | (col8 == 2)) & low_y) | (((col8 == 6) | (col8 == 7)) & high_y)
    lane_sites = ((lane8 > 0) | low_y) & ((lane8 < LANES - 1) | high_y)
    lane_bonds = ((lane8 > 0) | low_y) & ((lane8 < LANES - 2) | (high_y & (lane8 < LANES - 1)))

    def keep(mask, value):
        return jnp.where(mask, value, 0.0)

    def level_one(e, beside, zs, z_sites, z_bonds, site_on, bond_on, sums):
        q, up, down = around_plane(e)
        nb = plane(beside)
        mine, six = strip_sum(s0, q, up, down)
        fresh = []
        for j in range(SITES):
            fresh.append(se[q, j] * mine[j] - scale * six[j])
            s1[q, j] = fresh[j]
        edges = edges_of(mine)
        if sums is None:
            for z in zs:
                mid, total_six = site_sum(v0, q, up, down, z, edges)
                v1[q, z + 3] = en[q, z + 3] * mid - scale * total_six
            return None
        one, two, three, bond, right = zero, zero, zero, zero, zero
        t_one, t_two, t_three, t_bond = zero, zero, zero, zero
        for j in range(SITES):
            z_at = SITES * (slot8 - 1) + j
            in_sites = (z_at >= min(z_sites)) & (z_at <= max(z_sites))
            in_bonds = (z_at >= min(z_bonds)) & (z_at <= max(z_bonds))
            new = fresh[j]
            z_up = fresh[j + 1] if j + 1 < SITES else pltpu.roll(fresh[0], LANES - STRIP, 1)
            here = site_cols & in_sites
            square = new * new
            t_one = t_one + keep(here, mine[j] * new)
            t_two = t_two + keep(here, square)
            t_three = t_three + keep(here, se[q, j] * square)
            pairs = keep(site_cols & in_bonds, z_up) + keep(bond_cols & in_sites, pltpu.roll(new, LANES - 1, 1))
            t_three = t_three - (2.0 * scale) * (new * pairs)
            t_bond = t_bond + keep(here, new * s1[nb, j])
        before = None
        done = {}
        if min(z_bonds) < min(zs):
            done[min(z_bonds)] = v1[q, min(z_bonds) + 3]
        if max(z_bonds) + 1 > max(zs):
            done[max(z_bonds) + 1] = v1[q, max(z_bonds) + 4]
        for z in zs:
            mid, total_six = site_sum(v0, q, up, down, z, edges)
            energy = en[q, z + 3]
            new = energy * mid - scale * total_six
            v1[q, z + 3] = new
            if z in z_sites:
                square = new * new
                one, two, three = one + mid * new, two + square, three + energy * square
                right = right + new * pltpu.roll(new, LANES - 1, 1)
                bond = bond + new * v1[nb, z + 3]
            done[z] = new
            for at in (z - 1, z):
                if at in z_bonds and at in done and at + 1 in done:
                    three = three - (2.0 * scale) * (done[at] * done[at + 1])
        parts = (keep(lane_sites, one) + t_one, keep(lane_sites, two) + t_two,
                 keep(lane_sites, three) + t_three - (2.0 * scale) * keep(lane_bonds, right))
        bond = (-2.0 * scale) * (keep(lane_sites, bond) + t_bond)
        parts = tuple(jnp.where(site_on, part, 0.0) for part in parts)
        bond = jnp.where(bond_on, bond, 0.0)
        return sums[0] + parts[0], sums[1] + parts[1], sums[2] + parts[2] + bond

    def inner_planes(zs, z_sites, z_bonds, sums):
        def body(e, sums):
            return level_one(e, e - 1, zs, z_sites, z_bonds, True, e > 1, sums)
        return lax.fori_loop(1, X - 1, body, sums)

    def outer_planes(zs, z_sites, z_bonds, sums):
        def body(i, sums):
            step = lax.rem(i, 3)
            upward = i < 3
            e = jnp.where(upward, X - 1 + step, -step)
            on = (upward & high_x) | (jnp.logical_not(upward) & low_x)
            return level_one(e, jnp.where(upward, e - 1, e + 1), zs, z_sites, z_bonds, on & (step < 2), on, sums)
        return lax.fori_loop(0, 6, body, sums)

    def level_two(e, zs):
        q, up, down = around_plane(e)
        mine, sums = strip_sum(s1, q, up, down)
        for j in range(SITES):
            s2[q, j] = 2.0 * (se[q, j] * mine[j] - scale * sums[j]) - s0[q, j]
        edges = edges_of(mine)
        for z in zs:
            mid, total_six = site_sum(v1, q, up, down, z, edges)
            v2[q, z + 3] = 2.0 * (en[q, z + 3] * mid - scale * total_six) - v0[q, z + 3]

    def level_three(x, zs):
        q, up, down = around_plane(x)
        edges = edges_of([s2[q, j] for j in range(SITES)])
        for z in zs:
            mid, total_six = site_sum(v2, q, up, down, z, edges)
            new = 2.0 * (en[q, z + 3] * mid - scale * total_six) - v1[q, z + 3]
            at = pl.ds(x * Z + z, PROBES, stride=X * Z)
            prev_ref[at, :] = mid
            cur_ref[at, :] = new

    def levels_two_three(twos, threes):
        def two(i, _):
            level_two(i - 1, twos)
            return 0

        def three(x, _):
            level_three(x, threes)
            return 0

        lax.fori_loop(0, X + 2, two, 0)
        lax.fori_loop(0, X, three, 0)

    def send_moments(sums):
        row = zero
        for n, acc in enumerate(sums):
            summed = jnp.broadcast_to(jnp.sum(acc, axis=1, keepdims=True), (PROBES, LANES))
            row = row + jnp.where(lane8 == PROBES * n + probe, summed, 0.0)
        moms[me] = jnp.sum(row, axis=0, keepdims=True)
        each_other(lambda to: pltpu.make_async_remote_copy(
            src_ref=moms.at[me], dst_ref=moms.at[me], send_sem=msend_sem, recv_sem=mrecv_sem,
            device_id=to, device_id_type=MESH).start())

    def unpack_own(x, _):
        unpack(x, range(Z))
        return 0

    def unpack_far(i, _):
        unpack(plane(X + i), range(Z))
        return 0

    def unpack_low(i, _):
        unpack(plane(i - 3), range(Z))
        return 0

    lax.fori_loop(0, X, unpack_own, 0)
    for copy in groups["near"]:
        copy.wait_recv()
    strips[0] = join_strips(0, 1)
    unpack_strips(0)
    main = range(1, Z - 1)
    sums = inner_planes(main, main, range(1, Z - 2), (zero, zero, zero))
    for copy in groups["far"]:
        copy.wait_recv()
    for s in range(1, nbx):
        strips[s] = join_strips(s, 1)
        unpack_strips(s)
    if M <= X + 6:
        lax.fori_loop(0, M - X, unpack_far, 0)
    else:
        lax.fori_loop(0, 3, unpack_far, 0)
        lax.fori_loop(0, 3, unpack_low, 0)
    sums = outer_planes(main, main, range(1, Z - 2), sums)
    for n in range(3):
        accs[n] = sums[n]

    @pl.when(iz == last)
    def _():
        send_moments([accs[n] for n in range(3)])

    levels_two_three(range(2, Z - 2), range(3, Z - 3))

    if staged:
        @pl.when(iz == 0)
        def _():
            pl.semaphore_wait(token, per_plane)
            for copy in groups[-1]:
                copy.start()

    def side(up):
        for copy in groups[-1 if up else 1]:
            copy.wait_recv()
        outside = range(Z, Z + 3) if up else range(-3, 0)
        planes(3, 3, lambda q: unpack(q, outside))
        for s in range(nbx):
            if up:
                strips[s] = jnp.where(slot_word == W + 1, pltpu.roll(join_strips(s, 2), (STRIP * W) % LANES, 1), strips[s])
            else:
                strips[s] = jnp.where(slot_word == 0, pltpu.roll(join_strips(s, 0), (-STRIP * W) % LANES, 1), strips[s])
            unpack_strips(s)
        if up:
            ones, z_sites, z_bonds = range(Z - 1, Z + 2), range(Z - 1, Z + 1), range(Z - 2, Z + 1)
            twos, threes = range(Z - 2, Z + 1), range(Z - 3, Z)
        else:
            ones, z_sites, z_bonds = range(-2, 1), range(-1, 1), range(-2, 1)
            twos, threes = range(-1, 2), range(0, 3)
        sums = inner_planes(ones, z_sites, z_bonds, (zero, zero, zero))
        sums = outer_planes(ones, z_sites, z_bonds, sums)
        on = high_z if up else low_z
        for n in range(3):
            accs[n] = accs[n] + jnp.where(on, sums[n], 0.0)

        if up:
            @pl.when((iz > 0) & (iz < last))
            def _():
                send_moments([accs[n] for n in range(3)])
        else:
            @pl.when(iz == 0)
            def _():
                send_moments([accs[n] for n in range(3)])
        levels_two_three(twos, threes)

    @pl.when(iz == last)
    def _():
        side(False)

    side(True)

    @pl.when(iz < last)
    def _():
        side(False)

    others = moms.at[pl.ds(0, total - 1)]
    pltpu.make_async_copy(others, others, mrecv_sem).wait()
    sites = total * X * Z * LANES
    sums = jnp.sum(moms[...], axis=0) * (1.0 / sites)
    first = sums
    second = 2.0 * pltpu.roll(sums, LANES - PROBES, 1) - 1.0
    third = 4.0 * pltpu.roll(sums, LANES - 2 * PROBES, 1) - 3.0 * sums
    mom_ref[...] = jnp.concatenate([first, second, third], axis=0)[:, :PROBES]
    pltpu.make_async_copy(others, others, msend_sem).wait()
    for group in groups.values():
        for copy in group:
            copy.wait_send()


def write_out(mom_ref, prev_ref, cur_ref, mom_hbm, prev_hbm, cur_hbm, sem):
    copies = [pltpu.make_async_copy(src, dst, sem.at[n]) for n, (src, dst) in enumerate((
        (prev_ref, prev_hbm), (cur_ref, cur_hbm), (mom_ref, mom_hbm)))]
    for copy in copies:
        copy.start()
    for copy in copies:
        copy.wait()


def per_device(names, sizes, probe_bits, disorder_levels):
    X, W, Y = probe_bits.shape
    if Y != LANES or STRIP * (W + 2) > LANES or X < 3:
        raise ValueError("block size")
    Z = SITES * W
    nbx = 2 if sizes["gx"] == 2 else 3
    M = nbx * X
    n_copies = (9 * nbx - 1) + 2 * (3 * nbx - 1)
    total = sizes["gx"] * sizes["gy"] * sizes["gz"]
    rows = (X, W, 1, Y)
    vmem = pl.BlockSpec(memory_space=pltpu.VMEM)
    f32, i32 = jnp.float32, jnp.int32
    tile = (PROBES, LANES)
    hbm = pl.BlockSpec(memory_space=pltpu.HBM)
    out_shape = (
        jax.ShapeDtypeStruct((3, PROBES), f32),
        jax.ShapeDtypeStruct((PROBES * X * Z, Y), f32),
        jax.ShapeDtypeStruct((PROBES * X * Z, Y), f32),
    )
    results = pl.pallas_call(
        functools.partial(kernel, names, sizes),
        out_shape=out_shape,
        in_specs=[hbm] * 4,
        out_specs=(vmem,) * 3,
        scratch_shapes=[
            pltpu.VMEM((X, W, Y), i32),
            pltpu.VMEM((X, W, Y), i32),
            pltpu.VMEM((2, M, W + 2, 1, LANES), i32),
            pltpu.VMEM((nbx, 3, 3, 2 * X, LANES), i32),
            pltpu.VMEM((nbx, 2 * X, LANES), i32),
            pltpu.VMEM((M, Z + 6) + tile, f32),
            pltpu.VMEM((M, Z + 6) + tile, f32),
            pltpu.VMEM((M, Z + 6) + tile, f32),
            pltpu.VMEM((M, Z + 6) + tile, f32),
            pltpu.VMEM((M, SITES) + tile, f32),
            pltpu.VMEM((M, SITES) + tile, f32),
            pltpu.VMEM((M, SITES) + tile, f32),
            pltpu.VMEM((M, SITES) + tile, f32),
            pltpu.VMEM((3,) + tile, f32),
            pltpu.VMEM((total, 1, LANES), f32),
            pltpu.SemaphoreType.DMA((4,)),
            pltpu.SemaphoreType.DMA((n_copies,)),
            pltpu.SemaphoreType.DMA((n_copies,)),
            pltpu.SemaphoreType.DMA,
            pltpu.SemaphoreType.DMA,
            pltpu.SemaphoreType.REGULAR,
        ],
        compiler_params=pltpu.CompilerParams(collective_id=0, has_side_effects=True,
                                             vmem_limit_bytes=40 * 1024 * 1024),
    )(*[pltpu.with_memory_space_constraint(a, pltpu.HBM) for a in (probe_bits, disorder_levels, probe_bits.reshape(rows), disorder_levels.reshape(rows))])
    moments, previous, current = pl.pallas_call(
        write_out,
        out_shape=out_shape,
        in_specs=[vmem] * 3,
        out_specs=(hbm,) * 3,
        scratch_shapes=[pltpu.SemaphoreType.DMA((3,))],
        compiler_params=pltpu.CompilerParams(vmem_limit_bytes=16 * 1024 * 1024),
    )(*results)
    shape = (PROBES, X, Z, Y)
    return moments, previous.reshape(shape), current.reshape(shape)


def solution(mesh):
    placed = (P("gx", "gz", "gy"), P("gx", "gz", "gy"))
    sizes = {a: mesh.shape[a] for a in mesh.axis_names}
    return jax.shard_map(
        functools.partial(per_device, tuple(mesh.axis_names), sizes),
        mesh=mesh,
        in_specs=placed,
        out_specs=(P(), P(None, "gx", "gz", "gy"), P(None, "gx", "gz", "gy")),
        check_vma=False,
    )
```

time: 20.6 us -> 23.8 us (1.16)
  Pallas kernels: 19.7 us -> 22.9 us
    pallas_call x1, Pallas kernels: 18.7 us -> 21.9 us  [per_device(): pl.pallas_call(functools.partial(kernel, names, sizes), out_shape=out_sha...]
where the time goes in v1:
time: 23.8 us; the launch traced here: 23.5 us
  Pallas kernels  22.9 us (96%)
  between operations  0.64 us (3%)
    pallas_call x1, Pallas kernels, per_device(): pl.pallas_call(functools.partial(kernel, names, sizes), out_shape=out_sha...  21.9 us
    pallas_call x1, Pallas kernels, per_device(): pl.pallas_call(write_out, out_shape=out_shape, in_specs=[vmem] * 3, out_s...  1 us

profile of v1, /device:TPU:0, one launch (start us, length us, event | category | flops | bytes accessed | tf_op | source)
XLA Modules:
  0.0 23.5 jit_solution(8135702988967935429)
XLA Ops:
  0.6 21.9 %shard_map.49 = (f32[3,8]{1,0:T(4,128)S(1)}, f32[1024,128]{1,0:T(8,128)S(1)}, f32[1024,128]{1,0:T(8,128)S(1)}) custom-call(s32[4,8,128]{2,1,0:T(8,128)} %p_hbm.1, s32[4,8,128]{2,1,0:T(8,128)} %d_hbm.1, s32[4,8,1,128]{3,2,1,0:T(1,128)} %bitcast.4, s32[4,8,1,128]{3,2,1,0:T(1,128)} %bitcast.5), custom_call_target="tpu_custom_call" | custom-call | tf_op jit(solution)/shard_map/pallas_call | solution.py:505
  22.5 1.0 %shard_map.50 = (f32[3,8]{1,0:T(4,128)}, f32[1024,128]{1,0:T(8,128)}, f32[1024,128]{1,0:T(8,128)}) custom-call(f32[3,8]{1,0:T(4,128)S(1)} %get-tuple-element.9.mom_ref, f32[1024,128]{1,0:T(8,128)S(1)} %get-tuple-element.10.prev_ref, f32[1024,128]{1,0:T(8,128)S(1)} %get-tuple-element.11.cur_ref), custom_call_target="tpu_custom_call" | custom-call | tf_op jit(solution)/shard_map/pallas_call | solution.py:536

commit v2 on v1

v2 whole, which is shorter than its diff:
```python
import functools

import jax
import jax.numpy as jnp
from jax import lax
from jax.experimental import pallas as pl
from jax.experimental.pallas import tpu as pltpu
from jax.sharding import PartitionSpec as P

PROBES = 8
LEVELS = 256
LANES = 128
SITES = 4
STRIP = 12
PAD = 4

disorder_width = 4.0
spectral_scale = 8.4
MESH = pl.DeviceIdType.MESH


def kernel(names, sizes, p_hbm, d_hbm, prow_hbm, drow_hbm, mom_ref, prev_ref, cur_ref,
           p_ref, d_ref, words, packs, strips, v0, v1, v2, en, s0, s1, s2, se, accs, moms,
           load_sem, send_sem, recv_sem, msend_sem, mrecv_sem, above, entered):
    X, W, _ = p_ref.shape
    Z = SITES * W
    nbx = packs.shape[0]
    M = nbx * X
    gx, gy, gz = sizes["gx"], sizes["gy"], sizes["gz"]
    ix, iy, iz = (lax.axis_index(a) for a in ("gx", "gy", "gz"))
    total = gx * gy * gz
    me = (ix * gy + iy) * gz + iz
    last = gz - 1
    staged = gx <= 3 and gy <= 4 and 3 <= gz <= 4

    def device(x, y, z):
        at = {"gx": x, "gy": y, "gz": z}
        return tuple(at[a] for a in names)

    loads = [pltpu.make_async_copy(src, dst, load_sem.at[n]) for n, (src, dst) in enumerate((
        (p_hbm, p_ref), (d_hbm, d_ref),
        (prow_hbm, words.at[0, pl.ds(0, X), pl.ds(1, W)]), (drow_hbm, words.at[1, pl.ds(0, X), pl.ds(1, W)])))]
    for load in loads:
        load.start()

    def around(at, size):
        steps = [at]
        for _ in range(size - 1):
            steps.append(jnp.where(steps[-1] + 1 == size, 0, steps[-1] + 1))
        return steps

    around_x, around_y = around(ix, gx), around(iy, gy)

    def plane_of_others(z, act):
        for x in range(gx):
            for y in range(gy):
                if x or y:
                    act(device(around_x[x], around_y[y], z))

    def whole_plane(z, act):
        for x in range(gx):
            for y in range(gy):
                act(device(around_x[x], around_y[y], z))

    def each_other(act):
        if gz <= 4:
            for z in range(gz):
                @pl.when(iz != z)
                def _(z=z):
                    whole_plane(z, act)
        else:
            def step(n, _):
                whole_plane(lax.rem(iz + n, gz), act)
                return 0
            lax.fori_loop(1, gz, step, 0)
        plane_of_others(iz, act)

    xs = (0, 1) if nbx == 2 else (0, 1, -1)
    ys = (0, 1, -1)

    def at_offset(ox, oy, oz):
        return device(lax.rem(ix + ox + gx, gx), lax.rem(iy + oy + gy, gy), lax.rem(iz + oz + gz, gz))

    barrier = pltpu.get_barrier_semaphore()

    def greet(to):
        pl.semaphore_signal(barrier, inc=1, device_id=to, device_id_type=MESH)

    per_plane = len(xs) * len(ys)
    if staged:
        @pl.when(iz < last)
        def _():
            whole_plane(last, greet)
            for ox in xs:
                for oy in ys:
                    if ox or oy:
                        greet(at_offset(ox, oy, 0))

        @pl.when(iz == last)
        def _():
            plane_of_others(iz, greet)

        @pl.when(iz + 1 < last)
        def _():
            for ox in xs:
                for oy in ys:
                    greet(at_offset(ox, oy, 1))
    else:
        each_other(greet)

    lane = lax.broadcasted_iota(jnp.int32, (2 * X, LANES), 1)
    slot_word = (lane * 10923) >> 17
    column = lane - STRIP * slot_word

    for load in loads:
        load.wait()
    pack = jnp.zeros((2 * X, LANES), jnp.int32)
    for w in range(W):
        rows = jnp.concatenate([p_ref[:, w, :], d_ref[:, w, :]], axis=0)
        base = STRIP * (w + 1)
        first = pltpu.roll(rows, (base - (LANES - 3)) % LANES, 1)
        second = pltpu.roll(rows, (base + 5 - (LANES - 2)) % LANES, 1)
        pack = jnp.where(slot_word == w + 1, jnp.where(column < 5, first, second), pack)
    packs[0, 1, 1] = pack

    if staged:
        @pl.when(iz == last)
        def _():
            pl.semaphore_wait(barrier, total - 1)

        @pl.when(iz == 0)
        def _():
            pl.semaphore_wait(barrier, per_plane - 1)

        @pl.when((iz > 0) & (iz < last))
        def _():
            pl.semaphore_wait(barrier, 2 * per_plane - 1)
    else:
        pl.semaphore_wait(barrier, total - 1)

    slot_of = {0: 0, 1: nbx - 1, -1: 1}
    groups = {"far": [], "near": [], 1: [], -1: []}
    count = 0
    for oz in (0, 1, -1):
        for ox in xs:
            for oy in ys:
                if ox == 0 and oz == 0 and oy == 0:
                    continue
                s = slot_of[ox]
                moves = []
                if oy == 0:
                    src_w, dst_w = {0: (pl.ds(1, W), pl.ds(1, W)), 1: (pl.ds(W, 1), pl.ds(0, 1)),
                                    -1: (pl.ds(1, 1), pl.ds(W + 1, 1))}[oz]
                    for f in range(2):
                        moves.append((words.at[f, pl.ds(0, X), src_w], words.at[f, pl.ds(s * X, X), dst_w]))
                moves.append((packs.at[0, 1, 1], packs.at[s, 1 - oz, 1 - oy]))
                for src, dst in moves:
                    groups[oz if oz else ("far" if ox else "near")].append(pltpu.make_async_remote_copy(
                        src_ref=src, dst_ref=dst, send_sem=send_sem.at[count], recv_sem=recv_sem.at[count],
                        device_id=at_offset(ox, oy, oz), device_id_type=MESH))
                    count += 1

    def start(copies):
        for copy in copies:
            copy.start()

    def tell(semaphore, to):
        pl.semaphore_signal(semaphore, inc=1, device_id=to, device_id_type=MESH)

    if staged:
        @pl.when(iz == last)
        def _():
            start(groups[1])

        start(groups["far"] + groups["near"])

        @pl.when(iz > 0)
        def _():
            start(groups[-1])
            for ox in xs:
                for oy in ys:
                    tell(above, at_offset(ox, oy, -1))

        @pl.when(iz == last)
        def _():
            for z in range(last):
                tell(entered, device(ix, iy, z))
    else:
        start(groups[1] + groups["far"] + groups["near"] + groups[-1])

    e_mul = disorder_width / LEVELS
    e_add = disorder_width * (0.5 / LEVELS - 0.5)
    two_mul = 2.0 / (spectral_scale * spectral_scale)
    three_mul = 2.0 / spectral_scale
    one_mul = 1.0 / spectral_scale
    probe = lax.broadcasted_iota(jnp.int32, (PROBES, LANES), 0)
    lane8 = lax.broadcasted_iota(jnp.int32, (PROBES, LANES), 1)
    slot8 = (lane8 * 10923) >> 17
    col8 = lane8 - STRIP * slot8
    lifts = [31 - (SITES * probe + j) for j in range(SITES)]
    zero = jnp.zeros((PROBES, LANES), jnp.float32)

    def sign_of(row, j):
        return jnp.where((jnp.broadcast_to(row, (PROBES, LANES)) << lifts[j]) < 0, 1.0, -1.0).astype(jnp.float32)

    def energy_of(row, j):
        level = (jnp.broadcast_to(row, (PROBES, LANES)) >> (8 * j)) & 255
        return level.astype(jnp.float32) * e_mul + e_add

    def unpack(q, zs):
        for z in zs:
            w, j = divmod(z + SITES, SITES)
            v0[q, z + SITES] = sign_of(words[0, q, w], j)
            en[q, z + SITES] = energy_of(words[1, q, w], j)

    def plane(e):
        return lax.rem(e + M, M)

    def planes(low, high, body):
        def step(i, _):
            body(plane(i - low))
            return 0
        lax.fori_loop(0, min(M, X + low + high), step, 0)

    def join_strips(s, oz):
        return jnp.where(column < 3, packs[s, oz, 0], jnp.where(column < 7, packs[s, oz, 1], packs[s, oz, 2]))

    def unpack_strips(s):
        for x in range(X):
            for j in range(SITES):
                s0[s * X + x, j] = sign_of(strips[s, x:x + 1], j)
                se[s * X + x, j] = energy_of(strips[s, X + x:X + x + 1], j)

    def strip_sum(src, q, up, down):
        mine = [src[q, j] for j in range(SITES)]
        sums, rights, ups = [], [], []
        for j in range(SITES):
            z_up = mine[j + 1] if j + 1 < SITES else pltpu.roll(mine[0], LANES - STRIP, 1)
            z_down = mine[j - 1] if j > 0 else pltpu.roll(mine[SITES - 1], STRIP, 1)
            sums.append(src[up, j] + src[down, j] + pltpu.roll(mine[j], LANES - 1, 1)
                        + pltpu.roll(mine[j], 1, 1) + z_up + z_down)
        return mine, sums

    def edges_of(mine):
        return [jnp.where(col8 == 1, pltpu.roll(m, LANES - 6, 1), m) for m in mine]

    def site_sum(src, q, up, down, z, edges):
        w, j = divmod(z + SITES, SITES)
        fix = pltpu.roll(edges[j], (-(STRIP * w + 2)) % LANES, 1)
        mid = src[q, z + SITES]
        right = jnp.where(lane8 == LANES - 1, fix, pltpu.roll(mid, LANES - 1, 1))
        left = jnp.where(lane8 == 0, fix, pltpu.roll(mid, 1, 1))
        return mid, src[up, z + SITES] + src[down, z + SITES] + right + left + src[q, z + SITES + 1] + src[q, z + SITES - 1]

    def around_plane(e):
        return plane(e), plane(e + 1), plane(e + M - 1)

    def level_one(e, zs):
        q, up, down = around_plane(e)
        mine, six = strip_sum(s0, q, up, down)
        for j in range(SITES):
            s1[q, j] = se[q, j] * mine[j] - six[j]
        edges = edges_of(mine)
        for z in zs:
            mid, total_six = site_sum(v0, q, up, down, z, edges)
            v1[q, z + SITES] = en[q, z + SITES] * mid - total_six

    def level_two(e, zs, sums):
        q, up, down = around_plane(e)
        edges = edges_of([s1[q, j] for j in range(SITES)])
        for z in zs:
            mid, total_six = site_sum(v1, q, up, down, z, edges)
            start = v0[q, z + SITES]
            new = two_mul * (en[q, z + SITES] * mid - total_six) - start
            v2[q, z + SITES] = new
            if sums is not None:
                sums = sums[0] + start * mid, sums[1] + mid * mid, sums[2] + mid * new
        return sums

    def strip_two(x, _):
        q, up, down = around_plane(x)
        mine, six = strip_sum(s1, q, up, down)
        for j in range(SITES):
            s2[q, j] = two_mul * (se[q, j] * mine[j] - six[j]) - s0[q, j]
        return 0

    def level_three(x, zs):
        q, up, down = around_plane(x)
        edges = edges_of([s2[q, j] for j in range(SITES)])
        for z in zs:
            mid, total_six = site_sum(v2, q, up, down, z, edges)
            new = three_mul * (en[q, z + SITES] * mid - total_six) - one_mul * v1[q, z + SITES]
            at = pl.ds(x * Z + z, PROBES, stride=X * Z + PAD)
            prev_ref[at, :] = mid
            cur_ref[at, :] = new

    def loop(low, high, body):
        def step(i, _):
            body(i)
            return 0
        lax.fori_loop(low, high, step, 0)

    def own_two(zs):
        return lax.fori_loop(0, X, lambda x, sums: level_two(x, zs, sums), (zero, zero, zero))

    def send_moments(sums):
        row = zero
        for n, acc in enumerate(sums):
            summed = jnp.broadcast_to(jnp.sum(acc, axis=1, keepdims=True), (PROBES, LANES))
            row = row + jnp.where(lane8 == PROBES * n + probe, summed, 0.0)
        moms[me] = jnp.sum(row, axis=0, keepdims=True)
        each_other(lambda to: pltpu.make_async_remote_copy(
            src_ref=moms.at[me], dst_ref=moms.at[me], send_sem=msend_sem, recv_sem=mrecv_sem,
            device_id=to, device_id_type=MESH).start())

    def unpack_own(x, _):
        unpack(x, range(Z))
        return 0

    def unpack_far(i, _):
        unpack(plane(X + i), range(Z))
        return 0

    def unpack_low(i, _):
        unpack(plane(i - 3), range(Z))
        return 0

    lax.fori_loop(0, X, unpack_own, 0)
    for copy in groups["near"]:
        copy.wait_recv()
    strips[0] = join_strips(0, 1)
    unpack_strips(0)
    main = range(1, Z - 1)
    loop(1, X - 1, lambda x: level_one(x, main))
    for copy in groups["far"]:
        copy.wait_recv()
    for s in range(1, nbx):
        strips[s] = join_strips(s, 1)
        unpack_strips(s)
    if M <= X + 6:
        lax.fori_loop(0, M - X, unpack_far, 0)
    else:
        lax.fori_loop(0, 3, unpack_far, 0)
        lax.fori_loop(0, 3, unpack_low, 0)

    if staged:
        @pl.when(iz < last)
        def _():
            pl.semaphore_wait(above, per_plane)
            start(groups[1])

    def ends_of(low):
        width = X - 1 - 2 * low

        def body(i):
            level_one(low + i * width, main)
        return body

    loop(0, 2, ends_of(0))
    loop(0, 2, ends_of(-1))
    sums = own_two(range(2, Z - 2))
    for n in range(3):
        accs[n] = sums[n]

    @pl.when(iz == last)
    def _():
        send_moments([accs[n] for n in range(3)])

    loop(0, min(M, X + 4) - (X + 2), ends_of(-2))

    def side(up):
        for copy in groups[-1 if up else 1]:
            copy.wait_recv()
        outside = range(Z, Z + SITES) if up else range(-SITES, 0)
        planes(3, 3, lambda q: unpack(q, outside))
        for s in range(nbx):
            if up:
                strips[s] = jnp.where(slot_word == W + 1, pltpu.roll(join_strips(s, 2), (STRIP * W) % LANES, 1), strips[s])
            else:
                strips[s] = jnp.where(slot_word == 0, pltpu.roll(join_strips(s, 0), (-STRIP * W) % LANES, 1), strips[s])
            unpack_strips(s)
        ones = range(Z - 1, Z + 3) if up else range(-3, 1)
        twos = range(Z - 2, Z + 2) if up else range(-2, 2)
        loop(0, min(M, X + 4), lambda i: level_one(i - 2, ones))
        sums = own_two(twos)
        on = (iz != last) if up else (iz == 0)
        for n in range(3):
            accs[n] = accs[n] + jnp.where(on, sums[n], 0.0)

        if up:
            @pl.when((iz > 0) & (iz < last))
            def _():
                if staged:
                    pl.semaphore_wait(entered, 1)
                send_moments([accs[n] for n in range(3)])

            @pl.when(iz == 0)
            def _():
                if staged:
                    pl.semaphore_wait(entered, 1)
                    start(groups[-1])
        else:
            @pl.when(iz == 0)
            def _():
                send_moments([accs[n] for n in range(3)])

    @pl.when(iz == last)
    def _():
        side(False)

    side(True)

    @pl.when(iz < last)
    def _():
        side(False)

    loop(0, 2, lambda i: level_two(i * (X + 1) - 1, range(Z), None))
    lax.fori_loop(0, X, strip_two, 0)
    loop(0, X, lambda x: level_three(x, range(Z)))

    others = moms.at[pl.ds(0, total - 1)]
    pltpu.make_async_copy(others, others, mrecv_sem).wait()
    sites = total * X * Z * LANES
    sums = jnp.sum(moms[...], axis=0) * (1.0 / sites)
    first = one_mul * sums
    second = two_mul * pltpu.roll(sums, LANES - PROBES, 1) - 1.0
    third = three_mul * pltpu.roll(sums, LANES - 2 * PROBES, 1) - first
    mom_ref[...] = jnp.concatenate([first, second, third], axis=0)[:, :PROBES]
    pltpu.make_async_copy(others, others, msend_sem).wait()
    for group in groups.values():
        for copy in group:
            copy.wait_send()


def write_out(mom_ref, prev_ref, cur_ref, mom_hbm, prev_hbm, cur_hbm, sem):
    rows = prev_hbm.shape[0] // PROBES
    copies = [pltpu.make_async_copy(mom_ref, mom_hbm, sem.at[2 * PROBES])]
    for n, (src, dst) in enumerate(((prev_ref, prev_hbm), (cur_ref, cur_hbm))):
        for r in range(PROBES):
            copies.append(pltpu.make_async_copy(
                src.at[pl.ds(r * (rows + PAD), rows)], dst.at[pl.ds(r * rows, rows)], sem.at[n * PROBES + r]))
    for copy in copies:
        copy.start()
    for copy in copies:
        copy.wait()


def per_device(names, sizes, probe_bits, disorder_levels):
    X, W, Y = probe_bits.shape
    if Y != LANES or STRIP * (W + 2) > LANES or X < 3:
        raise ValueError("block size")
    Z = SITES * W
    nbx = 2 if sizes["gx"] == 2 else 3
    M = nbx * X
    n_copies = (9 * nbx - 1) + 2 * (3 * nbx - 1)
    total = sizes["gx"] * sizes["gy"] * sizes["gz"]
    rows = (X, W, 1, Y)
    vmem = pl.BlockSpec(memory_space=pltpu.VMEM)
    f32, i32 = jnp.float32, jnp.int32
    tile = (PROBES, LANES)
    hbm = pl.BlockSpec(memory_space=pltpu.HBM)
    out_shape = (
        jax.ShapeDtypeStruct((3, PROBES), f32),
        jax.ShapeDtypeStruct((PROBES * X * Z, Y), f32),
        jax.ShapeDtypeStruct((PROBES * X * Z, Y), f32),
    )
    padded = jax.ShapeDtypeStruct((PROBES * (X * Z + PAD), Y), f32)
    padded_shape = (out_shape[0], padded, padded)
    results = pl.pallas_call(
        functools.partial(kernel, names, sizes),
        out_shape=padded_shape,
        in_specs=[hbm] * 4,
        out_specs=(vmem,) * 3,
        scratch_shapes=[
            pltpu.VMEM((X, W, Y), i32),
            pltpu.VMEM((X, W, Y), i32),
            pltpu.VMEM((2, M, W + 2, 1, LANES), i32),
            pltpu.VMEM((nbx, 3, 3, 2 * X, LANES), i32),
            pltpu.VMEM((nbx, 2 * X, LANES), i32),
            pltpu.VMEM((M, Z + 2 * SITES) + tile, f32),
            pltpu.VMEM((M, Z + 2 * SITES) + tile, f32),
            pltpu.VMEM((M, Z + 2 * SITES) + tile, f32),
            pltpu.VMEM((M, Z + 2 * SITES) + tile, f32),
            pltpu.VMEM((M, SITES) + tile, f32),
            pltpu.VMEM((M, SITES) + tile, f32),
            pltpu.VMEM((M, SITES) + tile, f32),
            pltpu.VMEM((M, SITES) + tile, f32),
            pltpu.VMEM((3,) + tile, f32),
            pltpu.VMEM((total, 1, LANES), f32),
            pltpu.SemaphoreType.DMA((4,)),
            pltpu.SemaphoreType.DMA((n_copies,)),
            pltpu.SemaphoreType.DMA((n_copies,)),
            pltpu.SemaphoreType.DMA,
            pltpu.SemaphoreType.DMA,
            pltpu.SemaphoreType.REGULAR,
            pltpu.SemaphoreType.REGULAR,
        ],
        compiler_params=pltpu.CompilerParams(collective_id=0, has_side_effects=True,
                                             vmem_limit_bytes=40 * 1024 * 1024),
    )(*[pltpu.with_memory_space_constraint(a, pltpu.HBM) for a in (probe_bits, disorder_levels, probe_bits.reshape(rows), disorder_levels.reshape(rows))])
    moments, previous, current = pl.pallas_call(
        write_out,
        out_shape=out_shape,
        in_specs=[vmem] * 3,
        out_specs=(hbm,) * 3,
        scratch_shapes=[pltpu.SemaphoreType.DMA((2 * PROBES + 1,))],
        compiler_params=pltpu.CompilerParams(vmem_limit_bytes=16 * 1024 * 1024),
    )(*results)
    shape = (PROBES, X, Z, Y)
    return moments, previous.reshape(shape), current.reshape(shape)


def solution(mesh):
    placed = (P("gx", "gz", "gy"), P("gx", "gz", "gy"))
    sizes = {a: mesh.shape[a] for a in mesh.axis_names}
    return jax.shard_map(
        functools.partial(per_device, tuple(mesh.axis_names), sizes),
        mesh=mesh,
        in_specs=placed,
        out_specs=(P(), P(None, "gx", "gz", "gy"), P(None, "gx", "gz", "gy")),
        check_vma=False,
    )
```

time: 23.8 us -> 19.1 us (0.80)
  Pallas kernels: 22.9 us -> 18.2 us
    pallas_call x1, Pallas kernels: 21.9 us -> 17.1 us  [per_device(): pl.pallas_call(functools.partial(kernel, names, sizes), out_shape=padded_...]
where the time goes in v2:
time: 19.1 us; the launch traced here: 18.8 us
  Pallas kernels  18.2 us (95%)
  between operations  0.64 us (3%)
    pallas_call x1, Pallas kernels, per_device(): pl.pallas_call(functools.partial(kernel, names, sizes), out_shape=padded_...  17.1 us
    pallas_call x1, Pallas kernels, per_device(): pl.pallas_call(write_out, out_shape=out_shape, in_specs=[vmem] * 3, out_s...  1.1 us

profile of v2, /device:TPU:0, one launch (start us, length us, event | category | flops | bytes accessed | tf_op | source)
XLA Modules:
  0.0 18.8 jit_solution(6357281504950528557)
XLA Ops:
  0.6 17.1 %shard_map.49 = (f32[3,8]{1,0:T(4,128)S(1)}, f32[1056,128]{1,0:T(8,128)S(1)}, f32[1056,128]{1,0:T(8,128)S(1)}) custom-call(s32[4,8,128]{2,1,0:T(8,128)} %p_hbm.1, s32[4,8,128]{2,1,0:T(8,128)} %d_hbm.1, s32[4,8,1,128]{3,2,1,0:T(1,128)} %bitcast.4, s32[4,8,1,128]{3,2,1,0:T(1,128)} %bitcast.5), custom_call_target="tpu_custom_call" | custom-call | tf_op jit(solution)/shard_map/pallas_call | solution.py:469
  17.7 1.1 %shard_map.50 = (f32[3,8]{1,0:T(4,128)}, f32[1024,128]{1,0:T(8,128)}, f32[1024,128]{1,0:T(8,128)}) custom-call(f32[3,8]{1,0:T(4,128)S(1)} %get-tuple-element.9.mom_ref, f32[1056,128]{1,0:T(8,128)S(1)} %get-tuple-element.10.prev_ref, f32[1056,128]{1,0:T(8,128)S(1)} %get-tuple-element.11.cur_ref), custom_call_target="tpu_custom_call" | custom-call | tf_op jit(solution)/shard_map/pallas_call | solution.py:501

commit v3 on v2

v3 whole, which is shorter than its diff:
```python
import functools

import jax
import jax.numpy as jnp
from jax import lax
from jax.experimental import pallas as pl
from jax.experimental.pallas import tpu as pltpu
from jax.sharding import PartitionSpec as P

PROBES = 8
LEVELS = 256
LANES = 128
SITES = 4
STRIP = 12
PAD = 4
GROUP = 2

disorder_width = 4.0
spectral_scale = 8.4
MESH = pl.DeviceIdType.MESH


def kernel(names, sizes, p_hbm, d_hbm, prow_hbm, drow_hbm, mom_ref, prev_ref, cur_ref,
           p_ref, d_ref, words, packs, strips, v0, v1, v2, en, s0, s1, se, g0, g1, g2, moms, ruler,
           load_sem, send_sem, recv_sem, msend_sem, mrecv_sem, above, entered):
    X, W, _ = p_ref.shape
    Z = SITES * W
    nbx = packs.shape[0]
    M = nbx * X
    gx, gy, gz = sizes["gx"], sizes["gy"], sizes["gz"]
    ix, iy, iz = (lax.axis_index(a) for a in ("gx", "gy", "gz"))
    total = gx * gy * gz
    me = (ix * gy + iy) * gz + iz
    last = gz - 1
    staged = gx <= 3 and gy <= 4 and 3 <= gz <= 4

    def device(x, y, z):
        at = {"gx": x, "gy": y, "gz": z}
        return tuple(at[a] for a in names)

    loads = [pltpu.make_async_copy(src, dst, load_sem.at[n]) for n, (src, dst) in enumerate((
        (p_hbm, p_ref), (d_hbm, d_ref),
        (prow_hbm, words.at[0, pl.ds(0, X), pl.ds(1, W)]), (drow_hbm, words.at[1, pl.ds(0, X), pl.ds(1, W)])))]
    for load in loads:
        load.start()

    def around(at, size):
        steps = [at]
        for _ in range(size - 1):
            steps.append(jnp.where(steps[-1] + 1 == size, 0, steps[-1] + 1))
        return steps

    around_x, around_y = around(ix, gx), around(iy, gy)

    def plane_of_others(z, act):
        for x in range(gx):
            for y in range(gy):
                if x or y:
                    act(device(around_x[x], around_y[y], z))

    def each_other(act):
        def step(z, _):
            @pl.when(z != iz)
            def _():
                act(device(ix, iy, z))
            plane_of_others(z, act)
            return 0
        lax.fori_loop(0, gz, step, 0)

    xs = (0, 1) if nbx == 2 else (0, 1, -1)
    ys = (0, 1, -1)

    def at_offset(ox, oy, oz):
        return device(lax.rem(ix + ox + gx, gx), lax.rem(iy + oy + gy, gy), lax.rem(iz + oz + gz, gz))

    barrier = pltpu.get_barrier_semaphore()

    def tell(semaphore, to):
        pl.semaphore_signal(semaphore, inc=1, device_id=to, device_id_type=MESH)

    def greet(to):
        tell(barrier, to)

    per_plane = len(xs) * len(ys)
    if staged:
        plane_of_others(last, greet)

        @pl.when(iz < last)
        def _():
            greet(device(ix, iy, last))
            for ox in xs:
                for oy in ys:
                    if ox or oy:
                        greet(at_offset(ox, oy, 0))

        @pl.when(iz + 1 < last)
        def _():
            for ox in xs:
                for oy in ys:
                    greet(at_offset(ox, oy, 1))
    else:
        each_other(greet)

    lane = lax.broadcasted_iota(jnp.int32, (2 * X, LANES), 1)
    slot_word = (lane * 10923) >> 17
    column = lane - STRIP * slot_word

    for load in loads:
        load.wait()
    pack = jnp.zeros((2 * X, LANES), jnp.int32)
    for w in range(W):
        rows = jnp.concatenate([p_ref[:, w, :], d_ref[:, w, :]], axis=0)
        base = STRIP * (w + 1)
        first = pltpu.roll(rows, (base - (LANES - 3)) % LANES, 1)
        second = pltpu.roll(rows, (base + 5 - (LANES - 2)) % LANES, 1)
        pack = jnp.where(slot_word == w + 1, jnp.where(column < 5, first, second), pack)
    packs[0, 1, 1] = pack

    if staged:
        @pl.when(iz == last)
        def _():
            pl.semaphore_wait(barrier, total - 1)

        @pl.when(iz == 0)
        def _():
            pl.semaphore_wait(barrier, per_plane - 1)

        @pl.when((iz > 0) & (iz < last))
        def _():
            pl.semaphore_wait(barrier, 2 * per_plane - 1)
    else:
        pl.semaphore_wait(barrier, total - 1)

    slot_of = {0: 0, 1: nbx - 1, -1: 1}
    groups, lengths = [[] for _ in range(4)], [0] * 4
    near, far, rise, fall = range(4)
    for oz in (0, 1, -1):
        for ox in xs:
            for oy in ys:
                if ox == 0 and oz == 0 and oy == 0:
                    continue
                s = slot_of[ox]
                moves = []
                if oy == 0:
                    src_w, dst_w = {0: (pl.ds(1, W), pl.ds(1, W)), 1: (pl.ds(W, 1), pl.ds(0, 1)),
                                    -1: (pl.ds(1, 1), pl.ds(W + 1, 1))}[oz]
                    for f in range(2):
                        moves.append((words.at[f, pl.ds(0, X), src_w], words.at[f, pl.ds(s * X, X), dst_w],
                                      X * (W if oz == 0 else 1)))
                moves.append((packs.at[0, 1, 1], packs.at[s, 1 - oz, 1 - oy], 2 * X))
                g = {1: rise, -1: fall, 0: far if ox else near}[oz]
                for src, dst, length in moves:
                    lengths[g] += length
                    groups[g].append(pltpu.make_async_remote_copy(
                        src_ref=src, dst_ref=dst, send_sem=send_sem.at[g], recv_sem=recv_sem.at[g],
                        device_id=at_offset(ox, oy, oz), device_id_type=MESH))

    def start(g):
        for copy in groups[g]:
            copy.start()

    def arrive(sem, g):
        span = ruler.at[pl.ds(0, lengths[g])]
        pltpu.make_async_copy(span, span, sem).wait()

    if staged:
        @pl.when(iz == last)
        def _():
            start(rise)

        start(far)
        start(near)

        @pl.when(iz > 0)
        def _():
            start(fall)
            for ox in xs:
                for oy in ys:
                    tell(above, at_offset(ox, oy, -1))

        @pl.when(iz == last)
        def _():
            for z in range(last):
                tell(entered, device(ix, iy, z))
    else:
        for g in (rise, far, near, fall):
            start(g)

    e_mul = disorder_width / LEVELS
    e_add = disorder_width * (0.5 / LEVELS - 0.5)
    two_mul = 2.0 / (spectral_scale * spectral_scale)
    three_mul = 2.0 / spectral_scale
    one_mul = 1.0 / spectral_scale
    probe = lax.broadcasted_iota(jnp.int32, (PROBES, LANES), 0)
    lane8 = lax.broadcasted_iota(jnp.int32, (PROBES, LANES), 1)
    col8 = lane8 - STRIP * ((lane8 * 10923) >> 17)
    lifts = [31 - (SITES * probe + j) for j in range(SITES)]
    zero = jnp.zeros((PROBES, LANES), jnp.float32)

    def sign_of(row, j):
        return jnp.where((jnp.broadcast_to(row, (PROBES, LANES)) << lifts[j]) < 0, 1.0, -1.0).astype(jnp.float32)

    def energy_of(row, j):
        level = (jnp.broadcast_to(row, (PROBES, LANES)) >> (8 * j)) & 255
        return level.astype(jnp.float32) * e_mul + e_add

    def plane(e):
        return lax.rem(e + M, M)

    def around_plane(e):
        return plane(e), plane(e + 1), plane(e + M - 1)

    def loop(low, high, body):
        def step(i, _):
            body(i)
            return 0
        lax.fori_loop(low, high, step, 0)

    def edge_of(tile):
        return jnp.where(col8 == 1, pltpu.roll(tile, LANES - 6, 1), tile)

    def strip_sum(src, q, up, down):
        mine = [src[q, j] for j in range(SITES)]
        sums = []
        for j in range(SITES):
            z_up = mine[j + 1] if j + 1 < SITES else pltpu.roll(mine[0], LANES - STRIP, 1)
            z_down = mine[j - 1] if j > 0 else pltpu.roll(mine[SITES - 1], STRIP, 1)
            sums.append(src[up, j] + src[down, j] + pltpu.roll(mine[j], LANES - 1, 1)
                        + pltpu.roll(mine[j], 1, 1) + z_up + z_down)
        return mine, sums

    def rows_of(src, edges, q, up, down, w):
        fields = [src[q, SITES * w + r] for r in range(SITES * GROUP + 2)]
        for r in range(SITES * GROUP):
            row = SITES * w + r + 1
            turn = lax.rem(2 * LANES - 2 - STRIP * (w + r // SITES), LANES)
            fix = pltpu.roll(edges[q, r % SITES], turn, 1)
            mid = fields[r + 1]
            right = jnp.where(lane8 == LANES - 1, fix, pltpu.roll(mid, LANES - 1, 1))
            left = jnp.where(lane8 == 0, fix, pltpu.roll(mid, 1, 1))
            yield row, mid, src[up, row] + src[down, row] + right + left + fields[r + 2] + fields[r]

    def level_one(q, up, down, w):
        for row, mid, six in rows_of(v0, g0, q, up, down, w):
            v1[q, row] = en[q, row] * mid - six

    def level_two(q, up, down, w, first, final, sums):
        a, b, c = sums
        for row, mid, six in rows_of(v1, g1, q, up, down, w):
            begin = v0[q, row]
            new = two_mul * (en[q, row] * mid - six) - begin
            v2[q, row] = new
            counts = (row >= first) & (row <= final)
            part = jnp.where(counts, mid, 0.0)
            a, b, c = a + begin * part, b + part * part, c + part * jnp.where(counts, new, 0.0)
        return a, b, c

    def level_three(q, up, down, w):
        for n, (row, mid, six) in enumerate(rows_of(v2, g2, q, up, down, w)):
            at = pl.ds(q * Z + SITES * (w - 1) + n, PROBES, stride=X * Z + PAD)
            prev_ref[at, :] = mid
            cur_ref[at, :] = three_mul * (en[q, row] * mid - six) - one_mul * v1[q, row]

    def strip_one(e):
        q, up, down = around_plane(e)
        mine, six = strip_sum(s0, q, up, down)
        for j in range(SITES):
            new = se[q, j] * mine[j] - six[j]
            s1[q, j] = new
            g1[q, j] = edge_of(new)

    def strip_two(x):
        q, up, down = around_plane(x)
        mine, six = strip_sum(s1, q, up, down)
        for j in range(SITES):
            g2[q, j] = edge_of(two_mul * (se[q, j] * mine[j] - six[j]) - s0[q, j])

    def unpack_word(q, w):
        for j in range(SITES):
            row = SITES * w + j + 1
            v0[q, row] = sign_of(words[0, q, w], j)
            en[q, row] = energy_of(words[1, q, w], j)

    def unpack_strip(s, x):
        q = s * X + x
        for j in range(SITES):
            sign = sign_of(strips[s, pl.ds(x, 1)], j)
            s0[q, j] = sign
            g0[q, j] = edge_of(sign)
            se[q, j] = energy_of(strips[s, pl.ds(X + x, 1)], j)

    def send_moments(sums):
        row = zero
        for n, acc in enumerate(sums):
            summed = jnp.broadcast_to(jnp.sum(acc, axis=1, keepdims=True), (PROBES, LANES))
            row = row + jnp.where(lane8 == PROBES * n + probe, summed, 0.0)
        moms[me] = jnp.sum(row, axis=0, keepdims=True)
        each_other(lambda to: pltpu.make_async_remote_copy(
            src_ref=moms.at[me], dst_ref=moms.at[me], send_sem=msend_sem, recv_sem=mrecv_sem,
            device_id=to, device_id_type=MESH).start())

    def pick(n, values):
        chosen = values[-1]
        for m in range(len(values) - 1):
            chosen = jnp.where(n == m, values[m], chosen)
        return chosen

    def stage(n, sums):
        up = (n == 2) != (iz == last)
        inner = (n < 2) | (n == 4)

        @pl.when(n == 0)
        def _():
            arrive(recv_sem.at[near], near)

        @pl.when(n == 1)
        def _():
            arrive(recv_sem.at[far], far)
            if staged:
                @pl.when(iz < last)
                def _():
                    pl.semaphore_wait(above, per_plane)
                    start(rise)

        @pl.when(jnp.logical_not(inner) & up)
        def _():
            arrive(recv_sem.at[fall], fall)

        @pl.when(jnp.logical_not(inner) & jnp.logical_not(up))
        def _():
            arrive(recv_sem.at[rise], rise)

        side_word = jnp.where(up, W + 1, 0)
        slot_low = pick(n, (0, 1, 0, 0, nbx))
        slot_high = pick(n, (1, nbx))
        word_low = jnp.where(inner, 1, side_word)
        word_high = jnp.where(inner, W + 1, side_word + 1)
        which = jnp.where(inner, 1, jnp.where(up, 2, 0))
        turn = jnp.where(inner, 0, jnp.where(up, STRIP * W % LANES, (LANES - STRIP * W % LANES) % LANES))

        def unpack_slot(s):
            joined = jnp.where(column < 3, packs[s, which, 0], jnp.where(column < 7, packs[s, which, 1], packs[s, which, 2]))
            taken = jnp.broadcast_to(inner, slot_word.shape) | (slot_word == side_word)
            strips[s] = jnp.where(taken, pltpu.roll(joined, turn, 1), strips[s])

            def unpack_plane(x):
                unpack_strip(s, x)
                loop(word_low, word_high, lambda w: unpack_word(s * X + x, w))
            loop(0, X, unpack_plane)

        loop(slot_low, slot_high, unpack_slot)

        group_low = jnp.where(inner, 1, jnp.where(up, W + 1 - GROUP + 1, 0))
        groups_here = jnp.where(inner, W // GROUP, 1)

        def one(i):
            e = pick(n, (1, -1, -1, -1, -2)) + i + jnp.where(i >= pick(n, (X, 2, M, M, 1)), pick(n, (0, X - 2, 0, 0, X + 2)), 0)
            strip_one(e)
            at = around_plane(e)
            loop(0, groups_here, lambda g: level_one(*at, group_low + GROUP * g))

        loop(0, pick(n, (X - 2, 4, X + 2, X + 2, 2)), one)
        weigh = pick(n, (False, True, (iz != last) & up | (iz == 0) & jnp.logical_not(up), (iz != last) & up | (iz == 0) & jnp.logical_not(up), False))
        row_low = jnp.where(inner, 2, jnp.where(up, Z - 2, -2))
        row_high = jnp.where(weigh, jnp.where(inner, Z - 3, jnp.where(up, Z + 1, 1)), -Z)

        def two(i, sums):
            e = jnp.where(n == 4, (X + 1) * i - 1, i)
            at = around_plane(e)
            return lax.fori_loop(0, groups_here, lambda g, sums: level_two(
                *at, group_low + GROUP * g, row_low + SITES + 1, row_high + SITES + 1, sums), sums)

        sums = lax.fori_loop(0, pick(n, (0, X, X, X, 2)), two, sums)

        @pl.when(n == jnp.where(iz == last, 1, jnp.where(iz == 0, 3, 2)))
        def _():
            if staged:
                @pl.when((iz > 0) & (iz < last))
                def _():
                    pl.semaphore_wait(entered, 1)
            send_moments(sums)

        if staged:
            @pl.when((n == 2) & (iz == 0))
            def _():
                pl.semaphore_wait(entered, 1)
                start(fall)
        return sums

    lax.fori_loop(0, 5, stage, (zero, zero, zero))
    loop(0, X, strip_two)

    def three(x):
        at = around_plane(x)
        loop(0, W // GROUP, lambda g: level_three(*at, 1 + GROUP * g))

    loop(0, X, three)

    others = moms.at[pl.ds(0, total - 1)]
    pltpu.make_async_copy(others, others, mrecv_sem).wait()
    sites = total * X * Z * LANES
    sums = jnp.sum(moms[...], axis=0) * (1.0 / sites)
    first = one_mul * sums
    second = two_mul * pltpu.roll(sums, LANES - PROBES, 1) - 1.0
    third = three_mul * pltpu.roll(sums, LANES - 2 * PROBES, 1) - first
    mom_ref[...] = jnp.concatenate([first, second, third], axis=0)[:, :PROBES]
    pltpu.make_async_copy(others, others, msend_sem).wait()
    for g in range(4):
        arrive(send_sem.at[g], g)


def write_out(mom_ref, prev_ref, cur_ref, mom_hbm, prev_hbm, cur_hbm, sem):
    rows = prev_hbm.shape[0] // PROBES
    copies = [pltpu.make_async_copy(mom_ref, mom_hbm, sem.at[2 * PROBES])]
    for n, (src, dst) in enumerate(((prev_ref, prev_hbm), (cur_ref, cur_hbm))):
        for r in range(PROBES):
            copies.append(pltpu.make_async_copy(
                src.at[pl.ds(r * (rows + PAD), rows)], dst.at[pl.ds(r * rows, rows)], sem.at[n * PROBES + r]))
    for copy in copies:
        copy.start()
    for copy in copies:
        copy.wait()


def per_device(names, sizes, probe_bits, disorder_levels):
    X, W, Y = probe_bits.shape
    if Y != LANES or STRIP * (W + 2) > LANES or X < 3 or W % GROUP:
        raise ValueError("block size")
    Z = SITES * W
    nbx = 2 if sizes["gx"] == 2 else 3
    M = nbx * X
    total = sizes["gx"] * sizes["gy"] * sizes["gz"]
    rows = (X, W, 1, Y)
    vmem = pl.BlockSpec(memory_space=pltpu.VMEM)
    f32, i32 = jnp.float32, jnp.int32
    tile = (PROBES, LANES)
    hbm = pl.BlockSpec(memory_space=pltpu.HBM)
    out_shape = (
        jax.ShapeDtypeStruct((3, PROBES), f32),
        jax.ShapeDtypeStruct((PROBES * X * Z, Y), f32),
        jax.ShapeDtypeStruct((PROBES * X * Z, Y), f32),
    )
    padded = jax.ShapeDtypeStruct((PROBES * (X * Z + PAD), Y), f32)
    padded_shape = (out_shape[0], padded, padded)
    results = pl.pallas_call(
        functools.partial(kernel, names, sizes),
        out_shape=padded_shape,
        in_specs=[hbm] * 4,
        out_specs=(vmem,) * 3,
        scratch_shapes=[
            pltpu.VMEM((X, W, Y), i32),
            pltpu.VMEM((X, W, Y), i32),
            pltpu.VMEM((2, M, W + 2, 1, LANES), i32),
            pltpu.VMEM((nbx, 3, 3, 2 * X, LANES), i32),
            pltpu.VMEM((nbx, 2 * X, LANES), i32),
            pltpu.VMEM((M, Z + 2 * SITES + 2) + tile, f32),
            pltpu.VMEM((M, Z + 2 * SITES + 2) + tile, f32),
            pltpu.VMEM((M, Z + 2 * SITES + 2) + tile, f32),
            pltpu.VMEM((M, Z + 2 * SITES + 2) + tile, f32),
            pltpu.VMEM((M, SITES) + tile, f32),
            pltpu.VMEM((M, SITES) + tile, f32),
            pltpu.VMEM((M, SITES) + tile, f32),
            pltpu.VMEM((M, SITES) + tile, f32),
            pltpu.VMEM((M, SITES) + tile, f32),
            pltpu.VMEM((M, SITES) + tile, f32),
            pltpu.VMEM((total, 1, LANES), f32),
            pltpu.VMEM((X * (2 * W + 6) * nbx, LANES), i32),
            pltpu.SemaphoreType.DMA((4,)),
            pltpu.SemaphoreType.DMA((4,)),
            pltpu.SemaphoreType.DMA((4,)),
            pltpu.SemaphoreType.DMA,
            pltpu.SemaphoreType.DMA,
            pltpu.SemaphoreType.REGULAR,
            pltpu.SemaphoreType.REGULAR,
        ],
        compiler_params=pltpu.CompilerParams(collective_id=0, has_side_effects=True,
                                             vmem_limit_bytes=40 * 1024 * 1024),
    )(*[pltpu.with_memory_space_constraint(a, pltpu.HBM) for a in (probe_bits, disorder_levels, probe_bits.reshape(rows), disorder_levels.reshape(rows))])
    moments, previous, current = pl.pallas_call(
        write_out,
        out_shape=out_shape,
        in_specs=[vmem] * 3,
        out_specs=(hbm,) * 3,
        scratch_shapes=[pltpu.SemaphoreType.DMA((2 * PROBES + 1,))],
        compiler_params=pltpu.CompilerParams(vmem_limit_bytes=16 * 1024 * 1024),
    )(*results)
    shape = (PROBES, X, Z, Y)
    return moments, previous.reshape(shape), current.reshape(shape)


def solution(mesh):
    placed = (P("gx", "gz", "gy"), P("gx", "gz", "gy"))
    sizes = {a: mesh.shape[a] for a in mesh.axis_names}
    return jax.shard_map(
        functools.partial(per_device, tuple(mesh.axis_names), sizes),
        mesh=mesh,
        in_specs=placed,
        out_specs=(P(), P(None, "gx", "gz", "gy"), P(None, "gx", "gz", "gy")),
        check_vma=False,
    )
```

time: 19.1 us -> 26.2 us (1.37)
  the two profiles are of different devices: /device:TPU:0 before, /device:TPU:25 now
where the time goes in v3:
time: 26.2 us; the launch traced here: 25.9 us
  Pallas kernels  25.3 us (97%)
  between operations  0.64 us (2%)
    pallas_call x1, Pallas kernels, per_device(): pl.pallas_call(functools.partial(kernel, names, sizes), out_shape=padded_...  24.2 us
    pallas_call x1, Pallas kernels, per_device(): pl.pallas_call(write_out, out_shape=out_shape, in_specs=[vmem] * 3, out_s...  1.1 us

profile of v3, /device:TPU:25, one launch (start us, length us, event | category | flops | bytes accessed | tf_op | source)
XLA Modules:
  0.0 25.9 jit_solution(456475691437131631)
XLA Ops:
  0.6 24.2 %shard_map.49 = (f32[3,8]{1,0:T(4,128)S(1)}, f32[1056,128]{1,0:T(8,128)S(1)}, f32[1056,128]{1,0:T(8,128)S(1)}) custom-call(s32[4,8,128]{2,1,0:T(8,128)} %p_hbm.1, s32[4,8,128]{2,1,0:T(8,128)} %d_hbm.1, s32[4,8,1,128]{3,2,1,0:T(1,128)} %bitcast.4, s32[4,8,1,128]{3,2,1,0:T(1,128)} %bitcast.5), custom_call_target="tpu_custom_call" | custom-call | tf_op jit(solution)/shard_map/pallas_call | solution.py:445
  24.8 1.1 %shard_map.50 = (f32[3,8]{1,0:T(4,128)}, f32[1024,128]{1,0:T(8,128)}, f32[1024,128]{1,0:T(8,128)}) custom-call(f32[3,8]{1,0:T(4,128)S(1)} %get-tuple-element.9.mom_ref, f32[1056,128]{1,0:T(8,128)S(1)} %get-tuple-element.10.prev_ref, f32[1056,128]{1,0:T(8,128)S(1)} %get-tuple-element.11.cur_ref), custom_call_target="tpu_custom_call" | custom-call | tf_op jit(solution)/shard_map/pallas_call | solution.py:479

commit v4 on v2

--- a/solution.py
+++ b/solution.py
@@ -20,7 +20,7 @@
 
 
 def kernel(names, sizes, p_hbm, d_hbm, prow_hbm, drow_hbm, mom_ref, prev_ref, cur_ref,
-           p_ref, d_ref, words, packs, strips, v0, v1, v2, en, s0, s1, s2, se, accs, moms,
+           p_ref, d_ref, words, lefts, rights, packs, strips, v0, v1, v2, en, s0, s1, se, g1, g2, turned, accs, moms,
            load_sem, send_sem, recv_sem, msend_sem, mrecv_sem, above, entered):
     X, W, _ = p_ref.shape
     Z = SITES * W
@@ -225,11 +225,38 @@
     def join_strips(s, oz):
         return jnp.where(column < 3, packs[s, oz, 0], jnp.where(column < 7, packs[s, oz, 1], packs[s, oz, 2]))
 
+    def shift_words(s, ws):
+        own = pl.ds(s * X, X)
+        edges = jnp.where(column == 1, pltpu.roll(strips[s], LANES - 6, 1), strips[s])[:X]
+        for w in ws:
+            rows = words[0, own, w, 0, :]
+            fix = pltpu.roll(edges, (-(STRIP * w + 2)) % LANES, 1)
+            rights[own, w, 0, :] = jnp.where(lane[:X] == LANES - 1, fix, pltpu.roll(rows, LANES - 1, 1))
+            lefts[own, w, 0, :] = jnp.where(lane[:X] == 0, fix, pltpu.roll(rows, 1, 1))
+
     def unpack_strips(s):
+        for n, turn in enumerate((LANES - 1, 1, LANES - STRIP, STRIP)):
+            turned[s, n] = pltpu.roll(strips[s], turn, 1)
         for x in range(X):
             for j in range(SITES):
                 s0[s * X + x, j] = sign_of(strips[s, x:x + 1], j)
                 se[s * X + x, j] = energy_of(strips[s, X + x:X + x + 1], j)
+
+    def strip_one(q):
+        s, x = divmod(q, X)
+        for j in range(SITES):
+            right, left, z_up, z_down = (turned[s, n, x:x + 1] for n in range(4))
+            mine = s0[q, j]
+            six = (s0[(q + 1) % M, j] + s0[(q + M - 1) % M, j] + sign_of(right, j) + sign_of(left, j)
+                   + (s0[q, j + 1] if j + 1 < SITES else sign_of(z_up, 0))
+                   + (s0[q, j - 1] if j > 0 else sign_of(z_down, SITES - 1)))
+            new = se[q, j] * mine - six
+            s1[q, j] = new
+            g1[q, j] = edge_of(new)
+
+    def strips_one():
+        for q in sorted({e % M for e in range(-1, X + 1)}):
+            strip_one(q)
 
     def strip_sum(src, q, up, down):
         mine = [src[q, j] for j in range(SITES)]
@@ -241,12 +268,12 @@
                         + pltpu.roll(mine[j], 1, 1) + z_up + z_down)
         return mine, sums
 
-    def edges_of(mine):
-        return [jnp.where(col8 == 1, pltpu.roll(m, LANES - 6, 1), m) for m in mine]
+    def edge_of(tile):
+        return jnp.where(col8 == 1, pltpu.roll(tile, LANES - 6, 1), tile)
 
     def site_sum(src, q, up, down, z, edges):
         w, j = divmod(z + SITES, SITES)
-        fix = pltpu.roll(edges[j], (-(STRIP * w + 2)) % LANES, 1)
+        fix = pltpu.roll(edges[q, j], (-(STRIP * w + 2)) % LANES, 1)
         mid = src[q, z + SITES]
         right = jnp.where(lane8 == LANES - 1, fix, pltpu.roll(mid, LANES - 1, 1))
         left = jnp.where(lane8 == 0, fix, pltpu.roll(mid, 1, 1))
@@ -257,19 +284,17 @@
 
     def level_one(e, zs):
         q, up, down = around_plane(e)
-        mine, six = strip_sum(s0, q, up, down)
-        for j in range(SITES):
-            s1[q, j] = se[q, j] * mine[j] - six[j]
-        edges = edges_of(mine)
         for z in zs:
-            mid, total_six = site_sum(v0, q, up, down, z, edges)
-            v1[q, z + SITES] = en[q, z + SITES] * mid - total_six
+            w, j = divmod(z + SITES, SITES)
+            at = z + SITES
+            total_six = (v0[up, at] + v0[down, at] + sign_of(rights[q, w], j) + sign_of(lefts[q, w], j)
+                         + v0[q, at + 1] + v0[q, at - 1])
+            v1[q, at] = en[q, at] * v0[q, at] - total_six
 
     def level_two(e, zs, sums):
         q, up, down = around_plane(e)
-        edges = edges_of([s1[q, j] for j in range(SITES)])
         for z in zs:
-            mid, total_six = site_sum(v1, q, up, down, z, edges)
+            mid, total_six = site_sum(v1, q, up, down, z, g1)
             start = v0[q, z + SITES]
             new = two_mul * (en[q, z + SITES] * mid - total_six) - start
             v2[q, z + SITES] = new
@@ -277,18 +302,16 @@
                 sums = sums[0] + start * mid, sums[1] + mid * mid, sums[2] + mid * new
         return sums
 
-    def strip_two(x, _):
-        q, up, down = around_plane(x)
-        mine, six = strip_sum(s1, q, up, down)
-        for j in range(SITES):
-            s2[q, j] = two_mul * (se[q, j] * mine[j] - six[j]) - s0[q, j]
-        return 0
+    def strips_two():
+        for q in range(X):
+            mine, six = strip_sum(s1, q, q + 1, (q + M - 1) % M)
+            for j in range(SITES):
+                g2[q, j] = edge_of(two_mul * (se[q, j] * mine[j] - six[j]) - s0[q, j])
 
     def level_three(x, zs):
         q, up, down = around_plane(x)
-        edges = edges_of([s2[q, j] for j in range(SITES)])
         for z in zs:
-            mid, total_six = site_sum(v2, q, up, down, z, edges)
+            mid, total_six = site_sum(v2, q, up, down, z, g2)
             new = three_mul * (en[q, z + SITES] * mid - total_six) - one_mul * v1[q, z + SITES]
             at = pl.ds(x * Z + z, PROBES, stride=X * Z + PAD)
             prev_ref[at, :] = mid
@@ -329,6 +352,7 @@
     for copy in groups["near"]:
         copy.wait_recv()
     strips[0] = join_strips(0, 1)
+    shift_words(0, range(1, W + 1))
     unpack_strips(0)
     main = range(1, Z - 1)
     loop(1, X - 1, lambda x: level_one(x, main))
@@ -336,6 +360,7 @@
         copy.wait_recv()
     for s in range(1, nbx):
         strips[s] = join_strips(s, 1)
+        shift_words(s, range(1, W + 1))
         unpack_strips(s)
     if M <= X + 6:
         lax.fori_loop(0, M - X, unpack_far, 0)
@@ -356,6 +381,7 @@
             level_one(low + i * width, main)
         return body
 
+    strips_one()
     loop(0, 2, ends_of(0))
     loop(0, 2, ends_of(-1))
     sums = own_two(range(2, Z - 2))
@@ -378,11 +404,15 @@
                 strips[s] = jnp.where(slot_word == W + 1, pltpu.roll(join_strips(s, 2), (STRIP * W) % LANES, 1), strips[s])
             else:
                 strips[s] = jnp.where(slot_word == 0, pltpu.roll(join_strips(s, 0), (-STRIP * W) % LANES, 1), strips[s])
+            shift_words(s, [W + 1 if up else 0])
             unpack_strips(s)
         ones = range(Z - 1, Z + 3) if up else range(-3, 1)
         twos = range(Z - 2, Z + 2) if up else range(-2, 2)
+        strips_one()
         loop(0, min(M, X + 4), lambda i: level_one(i - 2, ones))
-        sums = own_two(twos)
+        sums = (zero, zero, zero)
+        for x in range(X):
+            sums = level_two(x, twos, sums)
         on = (iz != last) if up else (iz == 0)
         for n in range(3):
             accs[n] = accs[n] + jnp.where(on, sums[n], 0.0)
@@ -393,30 +423,37 @@
                 if staged:
                     pl.semaphore_wait(entered, 1)
                 send_moments([accs[n] for n in range(3)])
-
-            @pl.when(iz == 0)
-            def _():
-                if staged:
-                    pl.semaphore_wait(entered, 1)
-                    start(groups[-1])
         else:
             @pl.when(iz == 0)
             def _():
                 send_moments([accs[n] for n in range(3)])
 
+    def finish(zs):
+        loop(0, 2, lambda i: level_two(i * (X + 1) - 1, zs, None))
+        strips_two()
+        loop(0, X, lambda x: level_three(x, zs))
+
     @pl.when(iz == last)
     def _():
         side(False)
+        finish(range(Z - 3))
+
+    if staged:
+        @pl.when(iz == 0)
+        def _():
+            pl.semaphore_wait(entered, 1)
+            start(groups[-1])
 
     side(True)
+
+    @pl.when(iz == last)
+    def _():
+        finish(range(Z - 3, Z))
 
     @pl.when(iz < last)
     def _():
         side(False)
-
-    loop(0, 2, lambda i: level_two(i * (X + 1) - 1, range(Z), None))
-    lax.fori_loop(0, X, strip_two, 0)
-    loop(0, X, lambda x: level_three(x, range(Z)))
+        finish(range(Z))
 
     others = moms.at[pl.ds(0, total - 1)]
     pltpu.make_async_copy(others, others, mrecv_sem).wait()
@@ -475,6 +512,8 @@
             pltpu.VMEM((X, W, Y), i32),
             pltpu.VMEM((X, W, Y), i32),
             pltpu.VMEM((2, M, W + 2, 1, LANES), i32),
+            pltpu.VMEM((M, W + 2, 1, LANES), i32),
+            pltpu.VMEM((M, W + 2, 1, LANES), i32),
             pltpu.VMEM((nbx, 3, 3, 2 * X, LANES), i32),
             pltpu.VMEM((nbx, 2 * X, LANES), i32),
             pltpu.VMEM((M, Z + 2 * SITES) + tile, f32),
@@ -485,6 +524,8 @@
             pltpu.VMEM((M, SITES) + tile, f32),
             pltpu.VMEM((M, SITES) + tile, f32),
             pltpu.VMEM((M, SITES) + tile, f32),
+            pltpu.VMEM((M, SITES) + tile, f32),
+            pltpu.VMEM((nbx, 4, 2 * X, LANES), i32),
             pltpu.VMEM((3,) + tile, f32),
             pltpu.VMEM((total, 1, LANES), f32),
             pltpu.SemaphoreType.DMA((4,)),

time: 19.1 us -> 16.8 us (0.88)
  Pallas kernels: 18.2 us -> 15.9 us
    pallas_call x1, Pallas kernels: 17.1 us -> 14.8 us  [per_device(): pl.pallas_call(functools.partial(kernel, names, sizes), out_shape=padded_...]
where the time goes in v4:
time: 16.8 us; the launch traced here: 16.6 us
  Pallas kernels  15.9 us (95%)
  between operations  0.64 us (4%)
    pallas_call x1, Pallas kernels, per_device(): pl.pallas_call(functools.partial(kernel, names, sizes), out_shape=padded_...  14.8 us
    pallas_call x1, Pallas kernels, per_device(): pl.pallas_call(write_out, out_shape=out_shape, in_specs=[vmem] * 3, out_s...  1.1 us

profile of v4, /device:TPU:0, one launch (start us, length us, event | category | flops | bytes accessed | tf_op | source)
XLA Modules:
  0.0 16.6 jit_solution(16727117637045200390)
XLA Ops:
  0.6 14.8 %shard_map.49 = (f32[3,8]{1,0:T(4,128)S(1)}, f32[1056,128]{1,0:T(8,128)S(1)}, f32[1056,128]{1,0:T(8,128)S(1)}) custom-call(s32[4,8,128]{2,1,0:T(8,128)} %p_hbm.1, s32[4,8,128]{2,1,0:T(8,128)} %d_hbm.1, s32[4,8,1,128]{3,2,1,0:T(1,128)} %bitcast.4, s32[4,8,1,128]{3,2,1,0:T(1,128)} %bitcast.5), custom_call_target="tpu_custom_call" | custom-call | tf_op jit(solution)/shard_map/pallas_call | solution.py:506
  15.4 1.1 %shard_map.50 = (f32[3,8]{1,0:T(4,128)}, f32[1024,128]{1,0:T(8,128)}, f32[1024,128]{1,0:T(8,128)}) custom-call(f32[3,8]{1,0:T(4,128)S(1)} %get-tuple-element.9.mom_ref, f32[1056,128]{1,0:T(8,128)S(1)} %get-tuple-element.10.prev_ref, f32[1056,128]{1,0:T(8,128)S(1)} %get-tuple-element.11.cur_ref), custom_call_target="tpu_custom_call" | custom-call | tf_op jit(solution)/shard_map/pallas_call | solution.py:542

commit v5 on v4

--- a/solution.py
+++ b/solution.py
@@ -12,7 +12,7 @@
 LANES = 128
 SITES = 4
 STRIP = 12
-PAD = 4
+PAD = 8
 
 disorder_width = 4.0
 spectral_scale = 8.4
@@ -112,17 +112,8 @@
     slot_word = (lane * 10923) >> 17
     column = lane - STRIP * slot_word
 
-    for load in loads:
+    for load in loads[2:]:
         load.wait()
-    pack = jnp.zeros((2 * X, LANES), jnp.int32)
-    for w in range(W):
-        rows = jnp.concatenate([p_ref[:, w, :], d_ref[:, w, :]], axis=0)
-        base = STRIP * (w + 1)
-        first = pltpu.roll(rows, (base - (LANES - 3)) % LANES, 1)
-        second = pltpu.roll(rows, (base + 5 - (LANES - 2)) % LANES, 1)
-        pack = jnp.where(slot_word == w + 1, jnp.where(column < 5, first, second), pack)
-    packs[0, 1, 1] = pack
-
     if staged:
         @pl.when(iz == last)
         def _():
@@ -140,6 +131,7 @@
 
     slot_of = {0: 0, 1: nbx - 1, -1: 1}
     groups = {"far": [], "near": [], 1: [], -1: []}
+    split = {name: 0 for name in groups}
     count = 0
     for oz in (0, 1, -1):
         for ox in xs:
@@ -154,8 +146,11 @@
                     for f in range(2):
                         moves.append((words.at[f, pl.ds(0, X), src_w], words.at[f, pl.ds(s * X, X), dst_w]))
                 moves.append((packs.at[0, 1, 1], packs.at[s, 1 - oz, 1 - oy]))
-                for src, dst in moves:
-                    groups[oz if oz else ("far" if ox else "near")].append(pltpu.make_async_remote_copy(
+                for n, (src, dst) in enumerate(moves):
+                    group = oz if oz else ("far" if ox else "near")
+                    place = split[group] if n < len(moves) - 1 else len(groups[group])
+                    split[group] += n < len(moves) - 1
+                    groups[group].insert(place, pltpu.make_async_remote_copy(
                         src_ref=src, dst_ref=dst, send_sem=send_sem.at[count], recv_sem=recv_sem.at[count],
                         device_id=at_offset(ox, oy, oz), device_id_type=MESH))
                     count += 1
@@ -167,16 +162,52 @@
     def tell(semaphore, to):
         pl.semaphore_signal(semaphore, inc=1, device_id=to, device_id_type=MESH)
 
+    def first_of(group):
+        return groups[group][:split[group]]
+
+    def rest_of(group):
+        return groups[group][split[group]:]
+
+    if staged:
+        start(first_of("far"))
+
+        @pl.when(iz == last)
+        def _():
+            start(first_of(1))
+
+        @pl.when(iz > 0)
+        def _():
+            start(first_of(-1))
+    else:
+        for group in ("far", 1, -1):
+            start(first_of(group))
+
+    for load in loads[:2]:
+        load.wait()
+    pack = jnp.zeros((2 * X, LANES), jnp.int32)
+    for w in range(W):
+        rows = jnp.concatenate([p_ref[:, w, :], d_ref[:, w, :]], axis=0)
+        base = STRIP * (w + 1)
+        first = pltpu.roll(rows, (base - (LANES - 3)) % LANES, 1)
+        second = pltpu.roll(rows, (base + 5 - (LANES - 2)) % LANES, 1)
+        pack = jnp.where(slot_word == w + 1, jnp.where(column < 5, first, second), pack)
+    packs[0, 1, 1] = pack
+
     if staged:
         @pl.when(iz == last)
         def _():
-            start(groups[1])
-
-        start(groups["far"] + groups["near"])
+            start(rest_of(1))
+
+        start(rest_of("far"))
 
         @pl.when(iz > 0)
         def _():
-            start(groups[-1])
+            start(rest_of(-1))
+
+        start(groups["near"])
+
+        @pl.when(iz > 0)
+        def _():
             for ox in xs:
                 for oy in ys:
                     tell(above, at_offset(ox, oy, -1))
@@ -186,7 +217,8 @@
             for z in range(last):
                 tell(entered, device(ix, iy, z))
     else:
-        start(groups[1] + groups["far"] + groups["near"] + groups[-1])
+        for group in (1, "far", -1, "near"):
+            start(rest_of(group))
 
     e_mul = disorder_width / LEVELS
     e_add = disorder_width * (0.5 / LEVELS - 0.5)
@@ -225,18 +257,31 @@
     def join_strips(s, oz):
         return jnp.where(column < 3, packs[s, oz, 0], jnp.where(column < 7, packs[s, oz, 1], packs[s, oz, 2]))
 
-    def shift_words(s, ws):
+    def place_strips(s, oz):
+        joined = join_strips(s, oz)
         own = pl.ds(s * X, X)
-        edges = jnp.where(column == 1, pltpu.roll(strips[s], LANES - 6, 1), strips[s])[:X]
-        for w in ws:
+        side_slot = {0: 0, 1: None, 2: W + 1}[oz]
+        move = {0: -STRIP * W, 1: 0, 2: STRIP * W}[oz]
+
+        def put(ref, at, turn):
+            value = pltpu.roll(joined, (move + turn) % LANES, 1) if move + turn else joined
+            if side_slot is not None:
+                base = STRIP * side_slot + turn
+                value = jnp.where((lane >= base) & (lane < base + STRIP), value, ref[at])
+            ref[at] = value
+
+        put(strips, s, 0)
+        for n, turn in enumerate((-1, 1, -STRIP, STRIP)):
+            put(turned, (s, n), turn)
+        signs = joined[:X]
+        for w in range(1, W + 1) if oz == 1 else [side_slot]:
             rows = words[0, own, w, 0, :]
-            fix = pltpu.roll(edges, (-(STRIP * w + 2)) % LANES, 1)
-            rights[own, w, 0, :] = jnp.where(lane[:X] == LANES - 1, fix, pltpu.roll(rows, LANES - 1, 1))
-            lefts[own, w, 0, :] = jnp.where(lane[:X] == 0, fix, pltpu.roll(rows, 1, 1))
+            below = pltpu.roll(signs, (move - STRIP * w - 2) % LANES, 1)
+            above_it = pltpu.roll(signs, (move - STRIP * w - 8) % LANES, 1)
+            rights[own, w, 0, :] = jnp.where(lane[:X] == LANES - 1, above_it, pltpu.roll(rows, LANES - 1, 1))
+            lefts[own, w, 0, :] = jnp.where(lane[:X] == 0, below, pltpu.roll(rows, 1, 1))
 
     def unpack_strips(s):
-        for n, turn in enumerate((LANES - 1, 1, LANES - STRIP, STRIP)):
-            turned[s, n] = pltpu.roll(strips[s], turn, 1)
         for x in range(X):
             for j in range(SITES):
                 s0[s * X + x, j] = sign_of(strips[s, x:x + 1], j)
@@ -291,16 +336,31 @@
                          + v0[q, at + 1] + v0[q, at - 1])
             v1[q, at] = en[q, at] * v0[q, at] - total_six
 
-    def level_two(e, zs, sums):
+    def level_two(e, zs):
         q, up, down = around_plane(e)
         for z in zs:
             mid, total_six = site_sum(v1, q, up, down, z, g1)
-            start = v0[q, z + SITES]
-            new = two_mul * (en[q, z + SITES] * mid - total_six) - start
-            v2[q, z + SITES] = new
-            if sums is not None:
-                sums = sums[0] + start * mid, sums[1] + mid * mid, sums[2] + mid * new
-        return sums
+            v2[q, z + SITES] = two_mul * (en[q, z + SITES] * mid - total_six) - v0[q, z + SITES]
+
+    slot8 = (lane8 * 10923) >> 17
+
+    def moments_of(x, zs, sums):
+        q, up, down = around_plane(x)
+        one, two, three = sums
+        pair, rim = zero, zero
+        for z in zs:
+            at = z + SITES
+            mid = v1[q, at]
+            square = mid * mid
+            one, two = one + v0[q, at] * mid, two + square
+            three = three + en[q, at] * square - mid * (v1[up, at] + v1[down, at] + v1[q, at + 1] + v1[q, at - 1])
+            pair = pair + mid * pltpu.roll(mid, LANES - 1, 1)
+        for j in range(SITES):
+            z_at = SITES * (slot8 - 1) + j
+            mine = s1[q, j]
+            seam = ((col8 == 2) | (col8 == 6)) & (z_at >= min(zs)) & (z_at <= max(zs))
+            rim = rim + jnp.where(seam, mine * pltpu.roll(mine, LANES - 1, 1), 0.0)
+        return one, two, three - rim - jnp.where(lane8 < LANES - 1, 2.0 * pair, 0.0)
 
     def strips_two():
         for q in range(X):
@@ -323,8 +383,11 @@
             return 0
         lax.fori_loop(low, high, step, 0)
 
-    def own_two(zs):
-        return lax.fori_loop(0, X, lambda x, sums: level_two(x, zs, sums), (zero, zero, zero))
+    def own_moments(zs):
+        sums = (zero, zero, zero)
+        for x in range(X):
+            sums = moments_of(x, zs, sums)
+        return sums
 
     def send_moments(sums):
         row = zero
@@ -351,16 +414,14 @@
     lax.fori_loop(0, X, unpack_own, 0)
     for copy in groups["near"]:
         copy.wait_recv()
-    strips[0] = join_strips(0, 1)
-    shift_words(0, range(1, W + 1))
+    place_strips(0, 1)
     unpack_strips(0)
     main = range(1, Z - 1)
     loop(1, X - 1, lambda x: level_one(x, main))
     for copy in groups["far"]:
         copy.wait_recv()
     for s in range(1, nbx):
-        strips[s] = join_strips(s, 1)
-        shift_words(s, range(1, W + 1))
+        place_strips(s, 1)
         unpack_strips(s)
     if M <= X + 6:
         lax.fori_loop(0, M - X, unpack_far, 0)
@@ -384,15 +445,19 @@
     strips_one()
     loop(0, 2, ends_of(0))
     loop(0, 2, ends_of(-1))
-    sums = own_two(range(2, Z - 2))
+    middle = range(2, Z - 2)
+    sums = lax.fori_loop(0, X, lambda x, sums: moments_of(x, middle, sums), (zero, zero, zero))
     for n in range(3):
         accs[n] = sums[n]
+
+    def middle_rows():
+        loop(0, X, lambda x: level_two(x, middle))
+        loop(0, min(M, X + 4) - (X + 2), ends_of(-2))
 
     @pl.when(iz == last)
     def _():
         send_moments([accs[n] for n in range(3)])
-
-    loop(0, min(M, X + 4) - (X + 2), ends_of(-2))
+        middle_rows()
 
     def side(up):
         for copy in groups[-1 if up else 1]:
@@ -400,19 +465,13 @@
         outside = range(Z, Z + SITES) if up else range(-SITES, 0)
         planes(3, 3, lambda q: unpack(q, outside))
         for s in range(nbx):
-            if up:
-                strips[s] = jnp.where(slot_word == W + 1, pltpu.roll(join_strips(s, 2), (STRIP * W) % LANES, 1), strips[s])
-            else:
-                strips[s] = jnp.where(slot_word == 0, pltpu.roll(join_strips(s, 0), (-STRIP * W) % LANES, 1), strips[s])
-            shift_words(s, [W + 1 if up else 0])
+            place_strips(s, 2 if up else 0)
             unpack_strips(s)
         ones = range(Z - 1, Z + 3) if up else range(-3, 1)
         twos = range(Z - 2, Z + 2) if up else range(-2, 2)
         strips_one()
-        loop(0, min(M, X + 4), lambda i: level_one(i - 2, ones))
-        sums = (zero, zero, zero)
-        for x in range(X):
-            sums = level_two(x, twos, sums)
+        loop(0, X + 2, lambda i: level_one(i - 1, ones))
+        sums = own_moments(twos)
         on = (iz != last) if up else (iz == 0)
         for n in range(3):
             accs[n] = accs[n] + jnp.where(on, sums[n], 0.0)
@@ -423,20 +482,30 @@
                 if staged:
                     pl.semaphore_wait(entered, 1)
                 send_moments([accs[n] for n in range(3)])
+
+            @pl.when(iz < last)
+            def _():
+                middle_rows()
         else:
             @pl.when(iz == 0)
             def _():
                 send_moments([accs[n] for n in range(3)])
 
-    def finish(zs):
-        loop(0, 2, lambda i: level_two(i * (X + 1) - 1, zs, None))
+        outer = range(Z - 1, Z) if up else range(1)
+        loop(0, min(M, X + 4) - (X + 2), lambda i: level_one(i * (X + 3) - 2, outer))
+
+    def finish(twos, zs):
+        loop(0, X, lambda x: level_two(x, twos))
+        loop(0, 2, lambda i: level_two(i * (X + 1) - 1, zs))
         strips_two()
         loop(0, X, lambda x: level_three(x, zs))
+
+    bottom, top = [-1, 0, 1], [Z - 2, Z - 1, Z]
 
     @pl.when(iz == last)
     def _():
         side(False)
-        finish(range(Z - 3))
+        finish(bottom, range(Z - 3))
 
     if staged:
         @pl.when(iz == 0)
@@ -448,34 +517,32 @@
 
     @pl.when(iz == last)
     def _():
-        finish(range(Z - 3, Z))
+        finish(top, range(Z - 3, Z))
 
     @pl.when(iz < last)
     def _():
         side(False)
-        finish(range(Z))
-
+        finish(bottom + top, range(Z))
+
+    for group in groups.values():
+        for copy in group:
+            copy.wait_send()
     others = moms.at[pl.ds(0, total - 1)]
+    pltpu.make_async_copy(others, others, msend_sem).wait()
+    sites = total * X * Z * LANES
     pltpu.make_async_copy(others, others, mrecv_sem).wait()
-    sites = total * X * Z * LANES
     sums = jnp.sum(moms[...], axis=0) * (1.0 / sites)
     first = one_mul * sums
     second = two_mul * pltpu.roll(sums, LANES - PROBES, 1) - 1.0
-    third = three_mul * pltpu.roll(sums, LANES - 2 * PROBES, 1) - first
+    third = (three_mul * two_mul) * pltpu.roll(sums, LANES - 2 * PROBES, 1) - 3.0 * first
     mom_ref[...] = jnp.concatenate([first, second, third], axis=0)[:, :PROBES]
-    pltpu.make_async_copy(others, others, msend_sem).wait()
-    for group in groups.values():
-        for copy in group:
-            copy.wait_send()
 
 
 def write_out(mom_ref, prev_ref, cur_ref, mom_hbm, prev_hbm, cur_hbm, sem):
-    rows = prev_hbm.shape[0] // PROBES
-    copies = [pltpu.make_async_copy(mom_ref, mom_hbm, sem.at[2 * PROBES])]
-    for n, (src, dst) in enumerate(((prev_ref, prev_hbm), (cur_ref, cur_hbm))):
-        for r in range(PROBES):
-            copies.append(pltpu.make_async_copy(
-                src.at[pl.ds(r * (rows + PAD), rows)], dst.at[pl.ds(r * rows, rows)], sem.at[n * PROBES + r]))
+    rows = prev_hbm.shape[1]
+    inner = pl.ds(0, rows)
+    copies = [pltpu.make_async_copy(src, dst, sem.at[n]) for n, (src, dst) in enumerate((
+        (prev_ref.at[:, inner], prev_hbm), (cur_ref.at[:, inner], cur_hbm), (mom_ref, mom_hbm)))]
     for copy in copies:
         copy.start()
     for copy in copies:
@@ -498,8 +565,8 @@
     hbm = pl.BlockSpec(memory_space=pltpu.HBM)
     out_shape = (
         jax.ShapeDtypeStruct((3, PROBES), f32),
-        jax.ShapeDtypeStruct((PROBES * X * Z, Y), f32),
-        jax.ShapeDtypeStruct((PROBES * X * Z, Y), f32),
+        jax.ShapeDtypeStruct((PROBES, X * Z, Y), f32),
+        jax.ShapeDtypeStruct((PROBES, X * Z, Y), f32),
     )
     padded = jax.ShapeDtypeStruct((PROBES * (X * Z + PAD), Y), f32)
     padded_shape = (out_shape[0], padded, padded)
@@ -544,9 +611,9 @@
         out_shape=out_shape,
         in_specs=[vmem] * 3,
         out_specs=(hbm,) * 3,
-        scratch_shapes=[pltpu.SemaphoreType.DMA((2 * PROBES + 1,))],
+        scratch_shapes=[pltpu.SemaphoreType.DMA((3,))],
         compiler_params=pltpu.CompilerParams(vmem_limit_bytes=16 * 1024 * 1024),
-    )(*results)
+    )(results[0], *[a.reshape(PROBES, X * Z + PAD, Y) for a in results[1:]])
     shape = (PROBES, X, Z, Y)
     return moments, previous.reshape(shape), current.reshape(shape)
 

time: 16.8 us -> 16.4 us (0.976)
  Pallas kernels: 15.9 us -> 15.6 us
    pallas_call x1, Pallas kernels: 14.8 us -> 14.6 us  [per_device(): pl.pallas_call(functools.partial(kernel, names, sizes), out_shape=padded_...]
where the time goes in v5:
time: 16.4 us; the launch traced here: 16.3 us
  Pallas kernels  15.6 us (95%)
  between operations  0.64 us (4%)
    pallas_call x1, Pallas kernels, per_device(): pl.pallas_call(functools.partial(kernel, names, sizes), out_shape=padded_...  14.6 us
    pallas_call x1, Pallas kernels, per_device(): pl.pallas_call(write_out, out_shape=out_shape, in_specs=[vmem] * 3, out_s...  1 us

profile of v5, /device:TPU:0, one launch (start us, length us, event | category | flops | bytes accessed | tf_op | source)
XLA Modules:
  0.0 16.3 jit_solution(17789834374981168477)
XLA Ops:
  0.6 14.6 %shard_map.49 = (f32[3,8]{1,0:T(4,128)S(1)}, f32[1088,128]{1,0:T(8,128)S(1)}, f32[1088,128]{1,0:T(8,128)S(1)}) custom-call(s32[4,8,128]{2,1,0:T(8,128)} %p_hbm.1, s32[4,8,128]{2,1,0:T(8,128)} %d_hbm.1, s32[4,8,1,128]{3,2,1,0:T(1,128)} %bitcast.8, s32[4,8,1,128]{3,2,1,0:T(1,128)} %bitcast.9), custom_call_target="tpu_custom_call" | custom-call | tf_op jit(solution)/shard_map/pallas_call | solution.py:573
  15.3 1.0 %shard_map.50 = (f32[3,8]{1,0:T(4,128)}, f32[8,128,128]{2,1,0:T(8,128)}, f32[8,128,128]{2,1,0:T(8,128)}) custom-call(f32[3,8]{1,0:T(4,128)S(1)} %get-tuple-element.9.mom_ref, f32[8,136,128]{2,1,0:T(8,128)S(1)} %bitcast.6, f32[8,136,128]{2,1,0:T(8,128)S(1)} %bitcast.7), custom_call_target="tpu_custom_call" | custom-call | tf_op jit(solution)/shard_map/pallas_call | solution.py:609

commit v6 on v5

--- a/solution.py
+++ b/solution.py
@@ -88,17 +88,14 @@
 
     per_plane = len(xs) * len(ys)
     if staged:
+        for ox in xs:
+            for oy in ys:
+                if ox or oy:
+                    greet(at_offset(ox, oy, 0))
+
         @pl.when(iz < last)
         def _():
             whole_plane(last, greet)
-            for ox in xs:
-                for oy in ys:
-                    if ox or oy:
-                        greet(at_offset(ox, oy, 0))
-
-        @pl.when(iz == last)
-        def _():
-            plane_of_others(iz, greet)
 
         @pl.when(iz + 1 < last)
         def _():
@@ -117,7 +114,7 @@
     if staged:
         @pl.when(iz == last)
         def _():
-            pl.semaphore_wait(barrier, total - 1)
+            pl.semaphore_wait(barrier, total - 1 - (gx * gy - per_plane))
 
         @pl.when(iz == 0)
         def _():
@@ -214,8 +211,10 @@
 
         @pl.when(iz == last)
         def _():
-            for z in range(last):
-                tell(entered, device(ix, iy, z))
+            for z in range(last - 1):
+                for ox in xs:
+                    for oy in ys:
+                        tell(entered, at_offset(ox, oy, z + 1))
     else:
         for group in (1, "far", -1, "near"):
             start(rest_of(group))
@@ -423,6 +422,7 @@
     for s in range(1, nbx):
         place_strips(s, 1)
         unpack_strips(s)
+    strips_one()
     if M <= X + 6:
         lax.fori_loop(0, M - X, unpack_far, 0)
     else:
@@ -442,11 +442,13 @@
             level_one(low + i * width, main)
         return body
 
-    strips_one()
     loop(0, 2, ends_of(0))
     loop(0, 2, ends_of(-1))
     middle = range(2, Z - 2)
-    sums = lax.fori_loop(0, X, lambda x, sums: moments_of(x, middle, sums), (zero, zero, zero))
+    sums = lax.fori_loop(0, X // 2, lambda i, sums: moments_of(2 * i + 1, middle, moments_of(2 * i, middle, sums)),
+                         (zero, zero, zero))
+    if X % 2:
+        sums = moments_of(X - 1, middle, sums)
     for n in range(3):
         accs[n] = sums[n]
 
@@ -480,7 +482,9 @@
             @pl.when((iz > 0) & (iz < last))
             def _():
                 if staged:
-                    pl.semaphore_wait(entered, 1)
+                    @pl.when(iz < last - 1)
+                    def _():
+                        pl.semaphore_wait(entered, per_plane)
                 send_moments([accs[n] for n in range(3)])
 
             @pl.when(iz < last)
@@ -510,7 +514,7 @@
     if staged:
         @pl.when(iz == 0)
         def _():
-            pl.semaphore_wait(entered, 1)
+            pl.semaphore_wait(entered, per_plane)
             start(groups[-1])
 
     side(True)

time: 16.4 us -> 16.4 us (level)
  no operation moved by 1% of the time
where the time goes in v6:
time: 16.4 us; the launch traced here: 16.2 us
  Pallas kernels  15.6 us (95%)
  between operations  0.64 us (4%)
    pallas_call x1, Pallas kernels, per_device(): pl.pallas_call(functools.partial(kernel, names, sizes), out_shape=padded_...  14.6 us
    pallas_call x1, Pallas kernels, per_device(): pl.pallas_call(write_out, out_shape=out_shape, in_specs=[vmem] * 3, out_s...  1 us

profile of v6, /device:TPU:0, one launch (start us, length us, event | category | flops | bytes accessed | tf_op | source)
XLA Modules:
  0.0 16.2 jit_solution(5313552080618722300)
XLA Ops:
  0.6 14.6 %shard_map.49 = (f32[3,8]{1,0:T(4,128)S(1)}, f32[1088,128]{1,0:T(8,128)S(1)}, f32[1088,128]{1,0:T(8,128)S(1)}) custom-call(s32[4,8,128]{2,1,0:T(8,128)} %p_hbm.1, s32[4,8,128]{2,1,0:T(8,128)} %d_hbm.1, s32[4,8,1,128]{3,2,1,0:T(1,128)} %bitcast.8, s32[4,8,1,128]{3,2,1,0:T(1,128)} %bitcast.9), custom_call_target="tpu_custom_call" | custom-call | tf_op jit(solution)/shard_map/pallas_call | solution.py:577
  15.2 1.0 %shard_map.50 = (f32[3,8]{1,0:T(4,128)}, f32[8,128,128]{2,1,0:T(8,128)}, f32[8,128,128]{2,1,0:T(8,128)}) custom-call(f32[3,8]{1,0:T(4,128)S(1)} %get-tuple-element.9.mom_ref, f32[8,136,128]{2,1,0:T(8,128)S(1)} %bitcast.6, f32[8,136,128]{2,1,0:T(8,128)S(1)} %bitcast.7), custom_call_target="tpu_custom_call" | custom-call | tf_op jit(solution)/shard_map/pallas_call | solution.py:613

commit v7 on v6

--- a/solution.py
+++ b/solution.py
@@ -429,12 +429,6 @@
         lax.fori_loop(0, 3, unpack_far, 0)
         lax.fori_loop(0, 3, unpack_low, 0)
 
-    if staged:
-        @pl.when(iz < last)
-        def _():
-            pl.semaphore_wait(above, per_plane)
-            start(groups[1])
-
     def ends_of(low):
         width = X - 1 - 2 * low
 
@@ -451,6 +445,12 @@
         sums = moments_of(X - 1, middle, sums)
     for n in range(3):
         accs[n] = sums[n]
+
+    if staged:
+        @pl.when(iz < last)
+        def _():
+            pl.semaphore_wait(above, per_plane)
+            start(groups[1])
 
     def middle_rows():
         loop(0, X, lambda x: level_two(x, middle))

time: 16.4 us -> 16.4 us (level)
  no operation moved by 1% of the time
where the time goes in v7:
time: 16.4 us; the launch traced here: 16.2 us
  Pallas kernels  15.6 us (95%)
  between operations  0.64 us (4%)
    pallas_call x1, Pallas kernels, per_device(): pl.pallas_call(functools.partial(kernel, names, sizes), out_shape=padded_...  14.6 us
    pallas_call x1, Pallas kernels, per_device(): pl.pallas_call(write_out, out_shape=out_shape, in_specs=[vmem] * 3, out_s...  1 us

profile of v7, /device:TPU:0, one launch (start us, length us, event | category | flops | bytes accessed | tf_op | source)
XLA Modules:
  0.0 16.2 jit_solution(9962896211909056382)
XLA Ops:
  0.6 14.6 %shard_map.49 = (f32[3,8]{1,0:T(4,128)S(1)}, f32[1088,128]{1,0:T(8,128)S(1)}, f32[1088,128]{1,0:T(8,128)S(1)}) custom-call(s32[4,8,128]{2,1,0:T(8,128)} %p_hbm.1, s32[4,8,128]{2,1,0:T(8,128)} %d_hbm.1, s32[4,8,1,128]{3,2,1,0:T(1,128)} %bitcast.8, s32[4,8,1,128]{3,2,1,0:T(1,128)} %bitcast.9), custom_call_target="tpu_custom_call" | custom-call | tf_op jit(solution)/shard_map/pallas_call | solution.py:577
  15.2 1.0 %shard_map.50 = (f32[3,8]{1,0:T(4,128)}, f32[8,128,128]{2,1,0:T(8,128)}, f32[8,128,128]{2,1,0:T(8,128)}) custom-call(f32[3,8]{1,0:T(4,128)S(1)} %get-tuple-element.9.mom_ref, f32[8,136,128]{2,1,0:T(8,128)S(1)} %bitcast.6, f32[8,136,128]{2,1,0:T(8,128)S(1)} %bitcast.7), custom_call_target="tpu_custom_call" | custom-call | tf_op jit(solution)/shard_map/pallas_call | solution.py:613
